TPU v7x, 256 devices: a 8x8x2 block of a 8x8x16 slice. The times are simulated.
256 devices in a mesh: groups: 2 (over z), holders: 128 (over y, x, core).
Axes of the slice: x: 8, y: 8, z: 2, core: 2. Of those that a mesh axis runs over, the one named last changes fastest.
The devices are a block of a 8x8x16 slice.
Arguments:
- q_nope: bfloat16 [2, 256, 128], P(None, ('groups', 'holders')), parts along dimension 1, may hold values from -6 to 6
- q_rope: bfloat16 [2, 256, 64], P(None, ('groups', 'holders')), parts along dimension 1, may hold values from -30 to 30
- w_uk: bfloat16 [2, 16, 128, 512], replicated, may hold values from -0.5 to 0.5
- w_uv: bfloat16 [2, 16, 512, 128], replicated, may hold values from -0.25 to 0.25
- new_latent: bfloat16 [2, 16, 576], P(None, 'groups'), parts along dimension 1, may hold values from -33 to 33
- shallow_cache: bfloat16 [1, 256, 512, 576], P(None, ('groups', 'holders')), parts along dimension 1, may hold values from -30 to 30
- slot_positions: int32 [1, 256, 512], P(None, ('groups', 'holders')), parts along dimension 1, may hold values from 0 to 131071
- slab_map: int32 [1, 256], P(None, 'groups'), parts along dimension 1, may hold values from 0 to 127, each once within a row
- deep_cache: bfloat16 [1, 16, 256, 576], P(None, 'groups'), parts along dimension 1, may hold values from -30 to 30
- deep_positions: int32 [1, 16, 256], P(None, 'groups'), parts along dimension 1, may hold values from 0 to 131071
- lengths: int32 [16], P('groups'), parts along dimension 0, may hold values from 1 to 131072
Outputs:
- attended: bfloat16 [2, 256, 128], P(None, ('groups', 'holders')), parts along dimension 1
There are 2 independent parts, one for each index of `groups`. A program takes and returns all parts, laid end to end along the dimension named above; an argument that names none is the same for every part. Nothing has to cross between parts.
Inputs may be any that keep to these rules, and one draw needn't show every extreme that they name: Each row of slab_map names every slot once; entry b * 16 + s is the slot of request b's slab s.
All inputs are finite; a program needn't handle non-finite values.
Results may differ from a plain program's by a relative error of at most 0.0065.
Values may be sent and summed in bfloat16 or wider, within the bound.
No kernel may reach another device: no remote copies, remote signals or barrier semaphores. Data moves between devices by JAX's collectives and lax.ppermute only.
A program may use at most 64 MiB of HBM per device.

v0:
```python
import math

import jax
import jax.numpy as jnp
from jax import lax
from jax.sharding import Mesh
from jax.sharding import PartitionSpec as P

HEADS = 16
LATENT = 512
BATCH = 8
SLABS_REQ = 16
HOLDERS = ("holders_0", "holders_1", "holders_2")
GROUPS_HOLDERS = ("groups", "holders_0", "holders_1", "holders_2")


score_scale = 192.0 ** (-0.5)
neg_fill = -1e30


def copy_for_each(shard, axis):
    devices = lax.axis_size(axis)
    return lax.all_to_all(
        jnp.broadcast_to(shard[None], (devices, *shard.shape)), axis, 0, 0, tiled=True
    )


def joined_along(tiles, dim):
    dims = list(tiles.shape[1:])
    dims[dim] *= tiles.shape[0]
    return jnp.moveaxis(tiles, 0, dim).reshape(dims)


def gathered_by_axis(shard, axes, dim):
    far, near = axes
    tiles = copy_for_each(copy_for_each(shard, far), near)
    return joined_along(tiles.swapaxes(0, 1).reshape(-1, *shard.shape), dim)


def sent_together(arrays, axis, dim, along):
    widths = [a.shape[along] for a in arrays]
    both = jnp.concatenate(arrays, axis=along)
    filled = gathered_by_axis(both, axis, dim)
    return tuple(jnp.split(filled, [sum(widths[:k]) for k in range(1, len(widths))], axis=along))


def side_by_side(arrays, axis, split_dim, concat_dim, along):
    widths = [math.prod(a.shape[along:]) for a in arrays]
    both = jnp.concatenate(
        [a.reshape(*a.shape[:along], w) for a, w in zip(arrays, widths)], axis=along
    )
    filled = lax.all_to_all(both, axis, split_axis=split_dim, concat_axis=concat_dim, tiled=True)
    tiles = jnp.split(filled, [sum(widths[:k]) for k in range(1, len(widths))], axis=along)
    return tuple(
        (b.reshape(*filled.shape[:along], *a.shape[along:]) for a, b in zip(arrays, tiles))
    )


def block_partials(query_rows, keys, live):
    score = (
        jnp.einsum("nhc,ntc->nht", query_rows, keys, preferred_element_type=jnp.float32)
        * score_scale
    )
    block_max = jnp.max(jnp.where(live, score, neg_fill), axis=-1)
    weight = jnp.where(
        live, jnp.exp(jnp.where(live, score - block_max[..., None], 0.0)), 0.0
    ).astype(jnp.bfloat16)
    block_sum = jnp.sum(weight.astype(jnp.float32), axis=-1)
    block_out = jnp.einsum(
        "nht,ntc->nhc", weight, keys[..., :LATENT], preferred_element_type=jnp.float32
    )
    return (block_max, block_sum, block_out)


def shards(
    q_nope,
    q_rope,
    w_uk,
    w_uv,
    new_latent,
    shallow_cache,
    slot_positions,
    slab_map,
    deep_cache,
    deep_positions,
    lengths,
):
    rows_dev = q_nope.shape[1]
    holder_count = lax.axis_size(HOLDERS)
    start = lax.axis_index(HOLDERS) * rows_dev
    row_ids = start + jnp.arange(rows_dev, dtype=jnp.int32)
    head_ids = row_ids % HEADS
    row_req = row_ids // HEADS
    shallow_count = shallow_cache.shape[0]
    slot_dev = shallow_cache.shape[1]
    all_slots = slab_map.shape[1]
    per_req = max(1, rows_dev // HEADS)
    rows_req = rows_dev // per_req
    first_req = start // HEADS
    results = []
    for layer in range(q_nope.shape[0]):
        if layer < shallow_count:
            nope_all, rope_all = sent_together(
                (q_nope[layer], q_rope[layer]), (("holders_0", "holders_1"), "holders_2"), 0, 1
            )
            lat_all = jnp.einsum(
                "bhd,hdc->bhc",
                nope_all.reshape(BATCH, HEADS, -1),
                w_uk[layer],
                preferred_element_type=jnp.float32,
            ).astype(jnp.bfloat16)
            query_all = jnp.concatenate([lat_all, rope_all.reshape(BATCH, HEADS, -1)], axis=-1)
            query_own = lax.dynamic_slice_in_dim(
                query_all.reshape(BATCH * HEADS, -1), start, rows_dev, 0
            )
            slot_ids = lax.axis_index(HOLDERS) * slot_dev + jnp.arange(slot_dev, dtype=jnp.int32)
            owner_req = jnp.arange(all_slots, dtype=jnp.int32) // SLABS_REQ
            matches = slab_map[layer][None, :] == slot_ids[:, None]
            slot_req = jnp.sum(jnp.where(matches, owner_req[None, :], 0), axis=1)
            live = (slot_positions[layer] < lengths[slot_req][:, None])[:, None, :]
            slot_max, slot_sum, slot_out = block_partials(
                query_all[slot_req], shallow_cache[layer], live
            )
            chosen = slot_req[None, :] == jnp.arange(BATCH, dtype=jnp.int32)[:, None]
            dense_max = jnp.max(jnp.where(chosen[:, :, None], slot_max[None], neg_fill), axis=1)
            factor = jnp.where(
                chosen[:, :, None],
                jnp.exp(jnp.minimum(slot_max[None] - dense_max[:, None, :], 0.0)),
                0.0,
            )
            dense_sum = jnp.einsum("bjh,jh->bh", factor, slot_sum, precision=lax.Precision.HIGHEST)
            dense_out = jnp.einsum(
                "bjh,jhc->bhc", factor, slot_out, precision=lax.Precision.HIGHEST
            )
            flat_max = dense_max.reshape(-1)
            flat_sum = dense_sum.reshape(-1)
            flat_out = dense_out.reshape(BATCH * HEADS, -1)
            piece_max, piece_sum, piece_out = side_by_side(
                (
                    flat_max.reshape(holder_count, rows_dev),
                    flat_sum.reshape(holder_count, rows_dev),
                    flat_out.reshape(holder_count, rows_dev, -1),
                ),
                HOLDERS,
                0,
                0,
                2,
            )
            own_max = jnp.max(piece_max, axis=0)
            source_factor = jnp.exp(piece_max - own_max[None])
            own_sum = jnp.sum(piece_sum * source_factor, axis=0)
            own_out = jnp.sum(piece_out * source_factor[..., None], axis=0)
        else:
            own_lat = jnp.einsum(
                "rd,rdc->rc",
                q_nope[layer],
                w_uk[layer][head_ids],
                preferred_element_type=jnp.float32,
            ).astype(jnp.bfloat16)
            query_own = jnp.concatenate([own_lat, q_rope[layer]], axis=-1)
            deep_layer = layer - shallow_count
            deep_keys = lax.dynamic_slice_in_dim(deep_cache[deep_layer], first_req, per_req, 0)
            deep_where = lax.dynamic_slice_in_dim(deep_positions[deep_layer], first_req, per_req, 0)
            limits = lax.dynamic_slice_in_dim(lengths, first_req, per_req, 0)
            live = (deep_where < limits[:, None])[:, None, :]
            deep_max, deep_sum, deep_out = block_partials(
                query_own.reshape(per_req, rows_req, -1), deep_keys, live
            )
            own_max = deep_max.reshape(-1)
            own_sum = deep_sum.reshape(-1)
            own_out = deep_out.reshape(rows_dev, -1)
        newlat = new_latent[layer][row_req].astype(jnp.float32)
        own_score = jnp.sum(query_own.astype(jnp.float32) * newlat, axis=-1) * score_scale
        top = jnp.maximum(own_score, own_max)
        own_factor = jnp.exp(own_score - top)
        far_factor = jnp.exp(own_max - top)
        total = own_factor + own_sum * far_factor
        mixed = (
            (own_factor[:, None] * newlat[:, :LATENT] + own_out * far_factor[:, None])
            / total[:, None]
        ).astype(jnp.bfloat16)
        attended = jnp.einsum(
            "rc,rcv->rv", mixed, w_uv[layer][head_ids], preferred_element_type=jnp.float32
        )
        results.append(attended.astype(jnp.bfloat16))
    return jnp.stack(results, axis=0)


def solution(mesh):
    finer = Mesh(
        mesh.devices.reshape(mesh.shape["groups"], 8, 8, 2),
        ("groups", "holders_0", "holders_1", "holders_2"),
    )
    in_specs = (
        P(None, GROUPS_HOLDERS, None),
        P(None, GROUPS_HOLDERS, None),
        P(),
        P(),
        P(None, "groups", None),
        P(None, GROUPS_HOLDERS, None, None),
        P(None, GROUPS_HOLDERS, None),
        P(None, "groups"),
        P(None, "groups", None, None),
        P(None, "groups", None),
        P("groups"),
    )
    out_specs = P(None, GROUPS_HOLDERS, None)
    return jax.shard_map(
        shards, mesh=finer, in_specs=in_specs, out_specs=out_specs, check_vma=False
    )
```

profile of v0, /device:TPU:513, one launch (start us, length us, event | category | flops | bytes accessed | tf_op | source)
XLA Modules:
  0.0 91.2 jit_solution(17772422924876895696)
XLA Ops:
  0.0 0.8 slice_bitcast_fusion.6
  0.8 0.7 slice_bitcast_fusion.5
  1.6 0.7 broadcast_in_dim.120
  2.2 21.8 %all-to-all-start = ((bf16[64,1,192]{2,1,0:T(2,128)(2,1)}), bf16[64,1,192]{2,1,0:T(2,128)(2,1)S(1)}, u32[]{:S(2)}, u32[]{:S(2)}) async-start(bf16[64,1,192]{2,1,0:T(2,128)(2,1)} %broadcast_in_dim.120), calls=%async_computation | async-start | bytes 131072 | tf_op jit(solution)/shard_map/all_to_all | solution.py:23
  24.1 1.4 %fusion.56 = s32[]{:T(128)} fusion(s32[1,128]{1,0:T(1,128)} %param.18, s32[]{:T(128)} %add.61), kind=kLoop, calls=%fused_computation.95 | loop fusion | flops 1407 | bytes 520 | tf_op jit(solution)/shard_map/reduce_sum | solution.py:119
  26.8 0.7 fusion.63
  27.5 1.6 %slice-done = bf16[1,16,128,512]{3,2,1,0:T(8,128)(2,1)S(1)} async-done(((bf16[2,16,128,512]{3,2,1,0:T(8,128)(2,1)}), bf16[1,16,128,512]{3,2,1,0:T(8,128)(2,1)S(1)}, s32[]{:S(2)}) %slice-start) | async-done | bytes 2097176 | tf_op jit(solution)/shard_map/slice | solution.py:157
  30.0 0.7 fusion.64
  30.7 1.4 %compare_reduce_fusion.1 = pred[256]{0:T(512)(128)(4,1)S(1)} fusion(s32[1,8,256]{2,1,0:T(8,128)} %param.20, s32[]{:T(128)S(6)} %select_n.125, s32[]{:T(128)} %bitcast.40), kind=kLoop, calls=%fused_computation.51 | loop fusion | flops 256 | bytes 1288 | tf_op jit(solution)/shard_map/lt | solution.py:165
  32.2 0.7 select_reduce_fusion.1
  32.9 1.4 %convert_reduce_fusion.1 = (f32[]{:T(128)}, bf16[256]{0:T(256)(128)(2,1)S(1)}) fusion(pred[256]{0:T(512)(128)(4,1)S(1)} %compare_reduce_fusion.1, f32[]{:T(128)} %select_reduce_fusion.1, f32[256]{0:T(256)S(1)} %bitcast.143), kind=kLoop, calls=%fused_computation.84 | loop fusion | flops 1791 | bytes 1800 | tf_op jit(solution)/shard_map/reduce_sum | solution.py:68
  34.3 4.6 %fusion.62 = (bf16[1,16,512,128]{3,2,1,0:T(8,128)(2,1)}, bf16[1,16,512,128]{3,2,1,0:T(8,128)(2,1)}) fusion(bf16[2,16,512,128]{3,2,1,0:T(8,128)(2,1)} %param.14), kind=kLoop, calls=%fused_computation.103 | loop fusion | bytes 8388608 | tf_op jit(solution)/shard_map/slice | solution.py:183
  38.9 0.8 compare_reduce_fusion
  39.6 0.2 fusion.17
  39.8 0.7 iota_compare_fusion
  40.6 8.5 %all_to_all.15 = bf16[2,64,1,192]{3,1,2,0:T(8,128)(2,1)S(1)} all-to-all(bf16[2,64,1,192]{3,1,2,0:T(8,128)(2,1)S(1)} %broadcast_in_dim.122), channel_id=1, replica_groups=mesh['groups'=2,'holders_0'=8,'holders_1'=8,'holders_2'=2] {'holders_2'}, dimensions={0} | all-to-all | bytes 98304 | tf_op jit(solution)/shard_map/all_to_all | solution.py:23
  49.3 2.0 %fusion.6 = bf16[8,16,512]{2,0,1:T(8,128)(2,1)S(1)} fusion(bf16[2,16,128,512]{3,2,1,0:T(8,128)(2,1)} %param.13, bf16[8,16,128]{2,1,0:T(8,128)(2,1)S(1)} %bitcast.140), kind=kOutput, calls=%fused_computation.4 | convolution fusion | flops 16842752 | bytes 2260992 | tf_op jit(solution)/shard_map/bhd,hdc->bhc/dot_general | solution.py:106
  51.3 0.3 select_reduce_fusion
  51.8 0.2 convert_reduce_fusion
  52.0 0.2 fusion.14
  52.6 0.2 pad_maximum_fusion
  52.8 1.1 %copy.40 = f32[128,1,514]{2,1,0:T(1,128)} copy(f32[128,1,514]{2,0,1:T(8,128)S(1)} %pad_maximum_fusion) | data formatting | bytes 526336 | tf_op jit(solution)/shard_map/concatenate | solution.py:49
  53.8 14.6 %all-to-all-start.2 = ((f32[128,1,514]{2,1,0:T(1,128)}), f32[128,1,514]{2,1,0:T(1,128)S(1)}, u32[]{:S(2)}, u32[]{:S(2)}) async-start(f32[128,1,514]{2,1,0:T(1,128)} %copy.40), calls=%async_computation.2 | async-start | bytes 655360 | tf_op jit(solution)/shard_map/all_to_all | solution.py:52
  68.4 0.7 multiply_reduce_fusion
  71.9 1.0 %fusion.10 = bf16[1,1,128]{2,1,0:T(2,128)(2,1)S(1)} fusion(bf16[1,16,512,128]{3,2,1,0:T(8,128)(2,1)} %get-tuple-element.91, s32[]{:T(128)} %bitcast.29, f32[1,512]{1,0:T(1,128)S(1)} %bitcast.146, f32[1,576]{1,0:T(1,128)S(1)} %get-tuple-element.89, f32[]{:T(128)} %bitcast.52, f32[]{:T(128)} %bitcast.44), kind=kOutput, calls=%fused_computation.8 | convolution fusion | flops 133248 | bytes 136960 | tf_op jit(solution)/shard_map/rc,rcv->rv/dot_general | solution.py:182
  73.0 0.6 multiply_reduce_fusion.1
  74.3 9.8 %all-to-all-done.2 = f32[128,1,514]{2,1,0:T(1,128)S(1)} async-done(((f32[128,1,514]{2,1,0:T(1,128)}), f32[128,1,514]{2,1,0:T(1,128)S(1)}, u32[]{:S(2)}, u32[]{:S(2)}) %all-to-all-start.2) | async-done | bytes 263200 | tf_op jit(solution)/shard_map/all_to_all | solution.py:52
  84.0 0.7 slice_reduce_fusion
  86.2 2.0 %fusion.27 = (f32[]{:T(128)}, f32[128]{0:T(128)S(1)}) fusion(f32[128,1,514]{2,1,0:T(1,128)S(1)} %all-to-all-done.2, f32[]{:T(128)} %slice_reduce_fusion), kind=kLoop, calls=%fused_computation.38 | loop fusion | flops 383 | bytes 1544 | tf_op jit(solution)/shard_map/reduce_sum | solution.py:151
  88.8 0.8 fusion.18
  89.6 1.0 %fusion.12 = bf16[1,1,128]{2,1,0:T(2,128)(2,1)S(1)} fusion(bf16[1,16,512,128]{3,2,1,0:T(8,128)(2,1)} %get-tuple-element.90, s32[]{:T(128)} %bitcast.29, f32[1,512]{1,0:T(1,128)S(1)} %bitcast.145, f32[1,576]{1,0:T(1,128)S(1)} %get-tuple-element.85, f32[]{:T(128)} %bitcast.28, f32[]{:T(128)} %bitcast.23), kind=kOutput, calls=%fused_computation.11 | convolution fusion | flops 133248 | bytes 136960 | tf_op jit(solution)/shard_map/rc,rcv->rv/dot_general | solution.py:182
  90.7 0.5 copy.41
  (37 shorter events, 1.2 us)
Async XLA Ops:
  0.0 30.0 %copy-start = (bf16[1,8,256,576]{2,3,1,0:T(8,128)(2,1)S(1)}, bf16[1,8,256,576]{2,3,1,0:T(8,128)(2,1)}, u32[]{:S(2)}) copy-start(bf16[1,8,256,576]{2,3,1,0:T(8,128)(2,1)} %param.19) | copy-start | bytes 7077892
  2.2 38.3 %all-to-all-start = ((bf16[64,1,192]{2,1,0:T(2,128)(2,1)}), bf16[64,1,192]{2,1,0:T(2,128)(2,1)S(1)}, u32[]{:S(2)}, u32[]{:S(2)}) async-start(bf16[64,1,192]{2,1,0:T(2,128)(2,1)} %broadcast_in_dim.120), calls=%async_computation | async-start | bytes 131072 | tf_op jit(solution)/shard_map/all_to_all | solution.py:23
  27.5 1.6 %slice-start = ((bf16[2,16,128,512]{3,2,1,0:T(8,128)(2,1)}), bf16[1,16,128,512]{3,2,1,0:T(8,128)(2,1)S(1)}, s32[]{:S(2)}) async-start(bf16[2,16,128,512]{3,2,1,0:T(8,128)(2,1)} %param.13), calls=%async_computation.3 | async-start | bytes 4194304 | tf_op jit(solution)/shard_map/slice | solution.py:157
  27.5 1.6 %copy-start.4 = (bf16[2,1,128]{2,0,1:T(2,128)(2,1)S(1)}, bf16[2,1,128]{2,0,1:T(2,128)(2,1)}, u32[]{:S(2)}) copy-start(bf16[2,1,128]{2,0,1:T(2,128)(2,1)} %param.11) | copy-start | bytes 1540
  27.5 2.5 %copy-start.2 = (s32[8]{0:T(128)S(1)}, s32[8]{0:T(128)}, u32[]{:S(2)}) copy-start(s32[8]{0:T(128)} %param.21) | copy-start | bytes 100
  34.3 4.6 %copy-start.3 = (s32[1,1,512]{2,1,0:T(1,128)S(1)}, s32[1,1,512]{2,1,0:T(1,128)}, u32[]{:S(2)}) copy-start(s32[1,1,512]{2,1,0:T(1,128)} %param.17) | copy-start | bytes 6148
  38.9 12.4 %copy-start.1 = (bf16[1,1,512,576]{2,3,1,0:T(8,128)(2,1)S(1)}, bf16[1,1,512,576]{2,3,1,0:T(8,128)(2,1)}, u32[]{:S(2)}) copy-start(bf16[1,1,512,576]{2,3,1,0:T(8,128)(2,1)} %param.16) | copy-start | bytes 1769476
  53.8 30.2 %all-to-all-start.2 = ((f32[128,1,514]{2,1,0:T(1,128)}), f32[128,1,514]{2,1,0:T(1,128)S(1)}, u32[]{:S(2)}, u32[]{:S(2)}) async-start(f32[128,1,514]{2,1,0:T(1,128)} %copy.40), calls=%async_computation.2 | async-start | bytes 655360 | tf_op jit(solution)/shard_map/all_to_all | solution.py:52
where the time goes:
time: 91.8 us; the launch traced here: 91.2 us
  starting transfers between devices  36.4 us (40%)
  local copies, waits for them, and re-layouts  11.9 us (13%)
  other arithmetic  11.9 us (13%)
  waiting for transfers between devices  9.78 us (11%)
  blocking collectives  8.53 us (9%)
  between operations  7.73 us (8%)
  matrix products  5.02 us (5%)
    all_to_all x1, starting transfers between devices, copy_for_each(): lax.all_to_all(jnp.broadcast_to(shard[None], (devices, *shard.shape)), ax...  21.8 us
    all_to_all x1, starting transfers between devices, side_by_side(): lax.all_to_all(both, axis, split_axis=split_dim, concat_axis=concat_dim,...  14.6 us
    all_to_all x1, waiting for transfers between devices, side_by_side(): lax.all_to_all(both, axis, split_axis=split_dim, concat_axis=concat_dim,...  9.78 us
    all_to_all x1, blocking collectives, copy_for_each(): lax.all_to_all(jnp.broadcast_to(shard[None], (devices, *shard.shape)), ax...  8.53 us
    slice x1, local copies, waits for them, and re-layouts, shards(): w_uv[layer][head_ids]  4.61 us
    dot_general x2, matrix products, shards(): jnp.einsum('rc,rcv->rv', mixed, w_uv[layer][head_ids], preferred_element_...  2.09 us
    reduce_sum x1, other arithmetic, shards(): own_sum = jnp.sum(piece_sum * source_factor, axis=0)  2.05 us
    dot_general x1, matrix products, shards(): jnp.einsum('bhd,hdc->bhc', nope_all.reshape(BATCH, HEADS, -1), w_uk[layer...  1.96 us
  transfers between devices with their start and end apart: 2, of which 1 were waited for; matrix products, arithmetic and copies ran while one was open for 17% of the time, Pallas kernels for 0%

commit v1 on v0

v1 whole, which is shorter than its diff:
```python
import jax
import jax.numpy as jnp
from jax import lax
from jax.experimental import pallas as pl
from jax.experimental.pallas import tpu as pltpu
from jax.sharding import PartitionSpec as P

HEADS = 16
LATENT = 512
SLABS_REQ = 16
LANES = 128
CHUNKS = LATENT // LANES
MSG = 8

score_scale = 192.0 ** (-0.5)
neg_fill = -1e30
f32 = jnp.float32
bf16 = jnp.bfloat16


def iota(shape, dim):
    return lax.broadcasted_iota(jnp.int32, shape, dim)


def nt_dot(a, b):
    return lax.dot_general(a, b, (((1,), (1,)), ((), ())), preferred_element_type=f32)


def nn_dot(a, b):
    return jnp.dot(a, b, preferred_element_type=f32)


def picked_row(rows, at):
    rows = rows.astype(f32)
    return jnp.sum(jnp.where(iota(rows.shape, 0) == at, rows, 0.0), axis=0, keepdims=True)


def prep_kernel(nope_ref, rope_ref, out_ref):
    nope = nope_ref[0, :1].astype(f32)
    rope = rope_ref[0, :1].astype(f32)
    rope = jnp.concatenate([rope, jnp.zeros((1, LANES - rope.shape[1]), f32)], axis=1)
    shape = (out_ref.shape[0], LANES)
    pair = jnp.where(iota(shape, 0) % 2 == 0, nope, rope)
    out_ref[...] = pair.astype(bf16)


def attend_kernel(
    idx_ref,
    lengths_ref,
    got_ref,
    nope_ref,
    rope_ref,
    w_uk_ref,
    w_uv_ref,
    newlat_ref,
    slab_ref,
    slab_pos_ref,
    map_ref,
    deep_ref,
    deep_pos_ref,
    send_ref,
    aux_ref,
):
    holder = idx_ref[0]
    own_req = holder // HEADS
    own_head = holder % HEADS

    owners = map_ref[...]
    place = iota(owners.shape, 1) // SLABS_REQ
    req_v = jnp.sum(jnp.where(owners == holder, place, 0), axis=1, keepdims=True)
    req = jnp.sum(req_v)

    rows = got_ref.shape[0]
    part = iota((2 * HEADS, rows), 0)
    want = (req_v * HEADS + part % HEADS) * 2 + part // HEADS
    pick = jnp.where(iota((2 * HEADS, rows), 1) == want, 1.0, 0.0).astype(bf16)
    q_all = nn_dot(pick, got_ref[...]).astype(bf16)
    rope_dim = rope_ref.shape[-1]
    q_nope, q_rope = q_all[:HEADS], q_all[HEADS:, :rope_dim]

    wide = jnp.concatenate([q_nope] * HEADS, axis=1)
    diagonal = iota(wide.shape, 1) // q_nope.shape[1] == iota(wide.shape, 0)
    wide = jnp.where(diagonal, wide, jnp.zeros_like(wide))
    w_uk = w_uk_ref[0].reshape(wide.shape[1], LATENT)
    q_lat = nn_dot(wide, w_uk).astype(bf16)

    latent = slab_ref[0, 0, :LATENT]
    rotary = slab_ref[0, 0, LATENT:]
    score = (nn_dot(q_lat, latent) + nn_dot(q_rope, rotary)) * score_scale
    live = slab_pos_ref[0] < lengths_ref[req]
    top = jnp.max(jnp.where(live, score, neg_fill), axis=1, keepdims=True)
    weight = jnp.where(live, jnp.exp(jnp.where(live, score - top, 0.0)), 0.0).astype(bf16)
    total = jnp.sum(weight.astype(f32), axis=1, keepdims=True)
    safe = jnp.where(total > 0.0, total, 1.0)
    out = nt_dot(weight, latent) / safe
    level = jnp.where(total > 0.0, top + jnp.log(safe), neg_fill)

    blocks = [out[:, j * LANES : (j + 1) * LANES].astype(bf16) for j in range(CHUNKS)]
    rest = jnp.broadcast_to(level, (HEADS, LANES))
    for _ in range(3):
        piece = rest.astype(bf16)
        blocks.append(piece)
        rest = rest - piece.astype(f32)
    stacked = jnp.concatenate(blocks, axis=0)
    shape = (HEADS * MSG, stacked.shape[0])
    line, column = iota(shape, 0), iota(shape, 1)
    place = (line % MSG) * HEADS + line // MSG
    spread = jnp.where((column == place) & (line % MSG < len(blocks)), 1.0, 0.0).astype(bf16)
    message = nn_dot(spread, stacked).astype(bf16)
    send_ref[pl.ds(pl.multiple_of(req * (HEADS * MSG), HEADS * MSG), HEADS * MSG), :] = message

    nope, rope = nope_ref[0], rope_ref[0]
    own_lat = nn_dot(nope[:1], w_uk_ref[0, own_head]).astype(bf16).astype(f32)
    newlat = picked_row(newlat_ref[0], own_req)
    own_score = (
        jnp.sum(own_lat * newlat[:, :LATENT], axis=1, keepdims=True)
        + jnp.sum(rope[:1].astype(f32) * newlat[:, LATENT:], axis=1, keepdims=True)
    ) * score_scale
    for j in range(CHUNKS):
        aux_ref[j : j + 1, :] = newlat[:, j * LANES : (j + 1) * LANES]
    aux_ref[CHUNKS : CHUNKS + 1, :] = jnp.broadcast_to(own_score, (1, LANES))

    own_lat = nn_dot(nope[1:], w_uk_ref[1, own_head]).astype(bf16)
    latent = deep_ref[0, own_req, :LATENT]
    rotary = deep_ref[0, own_req, LATENT:]
    score = (nn_dot(own_lat, latent) + nn_dot(rope[1:], rotary)) * score_scale
    live = deep_pos_ref[0, pl.ds(own_req, 1), :] < lengths_ref[own_req]
    block_max = jnp.max(jnp.where(live, score, neg_fill), axis=1, keepdims=True)
    weight = jnp.where(live, jnp.exp(jnp.where(live, score - block_max, 0.0)), 0.0).astype(bf16)
    block_sum = jnp.sum(weight.astype(f32), axis=1, keepdims=True)
    block_out = nt_dot(weight, latent)
    newlat = picked_row(newlat_ref[1], own_req)
    own_score = (
        jnp.sum(own_lat.astype(f32) * newlat[:, :LATENT], axis=1, keepdims=True)
        + jnp.sum(rope[1:].astype(f32) * newlat[:, LATENT:], axis=1, keepdims=True)
    ) * score_scale
    top = jnp.maximum(own_score, block_max)
    own_factor = jnp.exp(own_score - top)
    far_factor = jnp.exp(block_max - top)
    total = own_factor + block_sum * far_factor
    mixed = ((own_factor * newlat[:, :LATENT] + block_out * far_factor) / total).astype(bf16)
    aux_ref[CHUNKS + 1 : CHUNKS + 2, :] = nn_dot(mixed, w_uv_ref[1, own_head])
    aux_ref[CHUNKS + 2 :, :] = jnp.zeros((MSG - CHUNKS - 2, LANES), f32)


def combine_kernel(idx_ref, map_ref, got_ref, aux_ref, w_uv_ref, out_ref):
    holder = idx_ref[0]
    own_req = holder // HEADS
    own_head = holder % HEADS
    own = aux_ref[...]
    own_score = own[CHUNKS : CHUNKS + 1]
    messages, levels = [], []
    top = own_score
    for s in range(SLABS_REQ):
        slot = map_ref[0, own_req * SLABS_REQ + s]
        message = got_ref[pl.ds(pl.multiple_of(slot * MSG, MSG), MSG), :].astype(f32)
        level = message[CHUNKS : CHUNKS + 1] + (
            message[CHUNKS + 1 : CHUNKS + 2] + message[CHUNKS + 2 : CHUNKS + 3]
        )
        messages.append(message)
        levels.append(level)
        top = jnp.maximum(top, level)
    total = jnp.exp(own_score - top)
    mixed = total * own
    for message, level in zip(messages, levels):
        factor = jnp.exp(level - top)
        total = total + factor
        mixed = mixed + factor * message
    mixed = (mixed / total).astype(bf16).astype(f32)
    row = jnp.concatenate([mixed[j : j + 1] for j in range(CHUNKS)], axis=1).astype(bf16)
    out = jnp.concatenate([nn_dot(row, w_uv_ref[0, own_head]), own[CHUNKS + 1 : CHUNKS + 2]], axis=0)
    out_ref[0] = out.astype(bf16)


VMEM = pl.BlockSpec(memory_space=pltpu.VMEM)
SMEM = pl.BlockSpec(memory_space=pltpu.SMEM)


def call(kernel, out_shape, in_specs, flops):
    many = isinstance(out_shape, tuple)
    return pl.pallas_call(
        kernel,
        out_shape=out_shape,
        in_specs=in_specs,
        out_specs=(VMEM,) * len(out_shape) if many else VMEM,
        compiler_params=pltpu.CompilerParams(vmem_limit_bytes=12 * 1024 * 1024),
        cost_estimate=pl.CostEstimate(flops=flops, bytes_accessed=1 << 20, transcendentals=0),
    )


def exchanged(rows, per_device):
    holders = lax.axis_size("holders")
    tiles = rows.reshape(holders, per_device, LANES)
    return lax.all_to_all(tiles, "holders", 0, 0, tiled=True).reshape(rows.shape)


def shards(
    q_nope,
    q_rope,
    w_uk,
    w_uv,
    new_latent,
    shallow_cache,
    slot_positions,
    slab_map,
    deep_cache,
    deep_positions,
    lengths,
):
    holders = lax.axis_size("holders")
    holder = lax.axis_index("holders").astype(jnp.int32).reshape(1)
    shape = jax.ShapeDtypeStruct
    q_nope, q_rope = q_nope.swapaxes(0, 1), q_rope.swapaxes(0, 1)
    shallow_cache, deep_cache = shallow_cache.swapaxes(2, 3), deep_cache.swapaxes(2, 3)
    queries = call(prep_kernel, shape((holders * 2, LANES), bf16), [VMEM] * 2, 1 << 33)(
        q_nope, q_rope
    )
    queries, holder = lax.optimization_barrier((queries, holder))
    queries = exchanged(queries, 2)
    partials, aux = call(
        attend_kernel,
        (shape((holders * MSG, LANES), bf16), shape((MSG, LANES), f32)),
        [SMEM, SMEM] + [VMEM] * 11,
        1 << 24,
    )(
        holder,
        lengths,
        queries,
        q_nope,
        q_rope,
        w_uk,
        w_uv,
        new_latent,
        shallow_cache,
        slot_positions,
        slab_map,
        deep_cache,
        deep_positions,
    )
    partials = exchanged(partials, MSG)
    rows = call(combine_kernel, shape(q_nope.shape, bf16), [SMEM, SMEM] + [VMEM] * 3, 1 << 20)(
        holder, slab_map, partials, aux, w_uv
    )
    return rows.swapaxes(0, 1)


def solution(mesh):
    spread = ("groups", "holders")
    in_specs = (
        P(None, spread, None),
        P(None, spread, None),
        P(),
        P(),
        P(None, "groups", None),
        P(None, spread, None, None),
        P(None, spread, None),
        P(None, "groups"),
        P(None, "groups", None, None),
        P(None, "groups", None),
        P("groups"),
    )
    return jax.shard_map(
        shards, mesh=mesh, in_specs=in_specs, out_specs=P(None, spread, None), check_vma=False
    )
```

time: 91.8 us -> 66.6 us (0.73)
  blocking collectives: 8.53 us -> 61.3 us
  starting transfers between devices: 36.4 us -> 0 us
  other arithmetic: 11.9 us -> 0 us
  local copies, waits for them, and re-layouts: 11.9 us -> 1.35 us
  waiting for transfers between devices: 9.78 us -> 0 us
  between operations: 7.73 us -> 0.11 us
  matrix products: 5.02 us -> 0 us
  Pallas kernels: 0 us -> 3.72 us
    all_to_all x1 -> x2, blocking collectives: 8.53 us -> 61.3 us  [exchanged(): lax.all_to_all(tiles, 'holders', 0, 0, tiled=True).reshape(rows.shape)]
    all_to_all x2 -> x0, starting transfers between devices: 36.4 us -> none  [the longest x1 21.8 us: copy_for_each(): lax.all_to_all(jnp.broadcast_to(shard[None], (devices, *shard.shape)), ax...]
    all_to_all x2 -> x0, waiting for transfers between devices: 9.78 us -> none  [the longest x1 9.78 us: side_by_side(): lax.all_to_all(both, axis, split_axis=split_dim, concat_axis=concat_dim,...]
    reduce_sum x7 -> x0, other arithmetic: 7.03 us -> none  [the longest x1 2.05 us: shards(): own_sum = jnp.sum(piece_sum * source_factor, axis=0)]
    slice x4 -> x0, local copies, waits for them, and re-layouts: 6.93 us -> none  [the longest x1 4.61 us: shards(): w_uv[layer][head_ids]]
    dot_general x8 -> x0, matrix products: 5.02 us -> none  [the longest x2 2.09 us: shards(): jnp.einsum('rc,rcv->rv', mixed, w_uv[layer][head_ids], preferred_element_...]
    pallas_call x0 -> x3, Pallas kernels: none -> 3.72 us  [the longest x1 2.44 us: shards(): call(attend_kernel, (shape((holders * MSG, LANES), bf16), shape((MSG, LAN...]
    lt x2 -> x0, other arithmetic: 2.11 us -> none  [the longest x1 1.35 us: shards(): live = (deep_where < limits[:, None])[:, None, :]]
  transfers between devices with their start and end apart: 2 -> 0, of which waited for: 1 -> 0; matrix products, arithmetic and copies ran while one was open for 17% -> 0% of each run, Pallas kernels for 0% -> 0%
where the time goes in v1:
time: 66.6 us; the launch traced here: 66.4 us
  blocking collectives  61.3 us (92%)
  Pallas kernels  3.72 us (6%)
  local copies, waits for them, and re-layouts  1.35 us (2%)
    all_to_all x2, blocking collectives, exchanged(): lax.all_to_all(tiles, 'holders', 0, 0, tiled=True).reshape(rows.shape)  61.3 us
    pallas_call x1, Pallas kernels, shards(): call(attend_kernel, (shape((holders * MSG, LANES), bf16), shape((MSG, LAN...  2.44 us
    unnamed x22, local copies, waits for them, and re-layouts  1.35 us

profile of v1, /device:TPU:513, one launch (start us, length us, event | category | flops | bytes accessed | tf_op | source)
XLA Modules:
  0.0 66.4 jit_solution(4600040816994943804)
XLA Ops:
  0.0 0.0 copy-start.9
  0.0 0.7 copy-done.9
  0.7 0.0 copy-start.10
  0.7 0.7 copy-done.10
  1.3 0.0 copy-start
  1.3 0.0 copy-start.1
  1.3 0.0 copy-start.2
  1.3 0.0 copy-start.3
  1.3 0.0 copy-start.4
  1.3 0.0 copy-start.5
  1.3 0.0 copy-start.6
  1.4 0.0 copy-start.7
  1.4 0.0 copy-start.8
  1.4 39.7 %all_to_all.10 = bf16[128,2,128]{2,1,0:T(2,128)(2,1)S(1)} all-to-all(bf16[128,2,128]{2,1,0:T(2,128)(2,1)S(1)} %bitcast.15), channel_id=1, replica_groups=mesh['groups'=2,'holders'=128] {'holders'}, dimensions={0} | all-to-all | bytes 131072 | tf_op jit(solution)/shard_map/all_to_all | solution.py:194
  41.1 0.0 copy-done
  41.1 0.0 copy-done.1
  41.1 0.0 copy-done.2
  41.1 0.0 copy-done.3
  41.1 0.0 copy-done.4
  41.1 0.0 copy-done.5
  41.1 0.0 copy-done.6
  41.1 0.0 copy-done.7
  41.1 0.0 copy-done.8
  41.2 2.4 %shard_map.110 = (bf16[1024,128]{1,0:T(8,128)(2,1)S(1)}, f32[8,128]{1,0:T(8,128)S(1)}) custom-call(s32[1]{0:T(128)} %bitcast.2.idx_ref, s32[8]{0:T(128)S(1)} %copy-done.8, bf16[256,128]{1,0:T(8,128)(2,1)S(1)} %bitcast.13, bf16[1,2,128]{2,1,0:T(2,128)(2,1)S(1)} %bitcast.17, bf16[1,2,64]{2,1,0:T(2,128)(2,1)S(1)} %bitcast.19, ...), custom_call_target="tpu_custom_call" | custom-call | flops 16777216 | bytes 1048576 | tf_op jit(solution)/shard_map/pallas_call | solution.py:220
  43.6 21.6 %all_to_all.11 = bf16[128,8,128]{2,1,0:T(8,128)(2,1)S(1)} all-to-all(bf16[128,8,128]{2,1,0:T(8,128)(2,1)S(1)} %bitcast.14), channel_id=1, replica_groups=mesh['groups'=2,'holders'=128] {'holders'}, dimensions={0} | all-to-all | bytes 524288 | tf_op jit(solution)/shard_map/all_to_all | solution.py:194
  65.2 1.2 %shard_map.111 = bf16[1,2,128]{2,1,0:T(2,128)(2,1)} custom-call(s32[1]{0:T(128)} %bitcast.2.idx_ref, s32[1,128]{1,0:T(1,128)S(1)} %copy-done.6, bf16[1024,128]{1,0:T(8,128)(2,1)S(1)} %bitcast.11, f32[8,128]{1,0:T(8,128)S(1)} %get-tuple-element.12.aux_ref, bf16[2,16,512,128]{3,2,1,0:T(8,128)(2,1)S(1)} %copy-done), custom_call_target="tpu_custom_call" | custom-call | flops 1048576 | bytes 1048576 | tf_op jit(solution)/shard_map/pallas_call | solution.py:241
  (1 shorter events, 0.0 us)
Async XLA Ops:
  0.0 0.7 copy-start.9
  0.7 0.7 copy-start.10
  1.3 39.8 %copy-start = (bf16[2,16,512,128]{3,2,1,0:T(8,128)(2,1)S(1)}, bf16[2,16,512,128]{3,2,1,0:T(8,128)(2,1)}, u32[]{:S(2)}) copy-start(bf16[2,16,512,128]{3,2,1,0:T(8,128)(2,1)} %w_uv_ref.3) | copy-start | bytes 12582916
  1.3 39.8 %copy-start.1 = (bf16[2,16,128,512]{3,2,1,0:T(8,128)(2,1)S(1)}, bf16[2,16,128,512]{3,2,1,0:T(8,128)(2,1)}, u32[]{:S(2)}) copy-start(bf16[2,16,128,512]{3,2,1,0:T(8,128)(2,1)} %w_uk_ref.1) | copy-start | bytes 12582916
  1.3 39.8 %copy-start.2 = (bf16[1,8,256,576]{2,3,1,0:T(8,128)(2,1)S(1)}, bf16[1,8,256,576]{2,3,1,0:T(8,128)(2,1)}, u32[]{:S(2)}) copy-start(bf16[1,8,256,576]{2,3,1,0:T(8,128)(2,1)} %param.19) | copy-start | bytes 7077892
  1.3 39.8 %copy-start.3 = (bf16[1,1,512,576]{2,3,1,0:T(8,128)(2,1)S(1)}, bf16[1,1,512,576]{2,3,1,0:T(8,128)(2,1)}, u32[]{:S(2)}) copy-start(bf16[1,1,512,576]{2,3,1,0:T(8,128)(2,1)} %param.16) | copy-start | bytes 1769476
  1.3 39.8 %copy-start.4 = (bf16[2,8,576]{2,1,0:T(8,128)(2,1)S(1)}, bf16[2,8,576]{2,1,0:T(8,128)(2,1)}, u32[]{:S(2)}) copy-start(bf16[2,8,576]{2,1,0:T(8,128)(2,1)} %newlat_ref.1) | copy-start | bytes 55300
  1.3 39.8 %copy-start.5 = (s32[1,8,256]{2,1,0:T(8,128)S(1)}, s32[1,8,256]{2,1,0:T(8,128)}, u32[]{:S(2)}) copy-start(s32[1,8,256]{2,1,0:T(8,128)} %deep_pos_ref.1) | copy-start | bytes 24580
  1.3 39.8 %copy-start.6 = (s32[1,128]{1,0:T(1,128)S(1)}, s32[1,128]{1,0:T(1,128)}, u32[]{:S(2)}) copy-start(s32[1,128]{1,0:T(1,128)} %map_ref.3) | copy-start | bytes 1540
  1.4 39.8 %copy-start.7 = (s32[1,1,512]{2,1,0:T(1,128)S(1)}, s32[1,1,512]{2,1,0:T(1,128)}, u32[]{:S(2)}) copy-start(s32[1,1,512]{2,1,0:T(1,128)} %slab_pos_ref.1) | copy-start | bytes 6148
  1.4 39.8 %copy-start.8 = (s32[8]{0:T(128)S(1)}, s32[8]{0:T(128)}, u32[]{:S(2)}) copy-start(s32[8]{0:T(128)} %lengths_ref.1) | copy-start | bytes 100

commit v2 on v1

--- a/solution.py
+++ b/solution.py
@@ -3,14 +3,17 @@
 from jax import lax
 from jax.experimental import pallas as pl
 from jax.experimental.pallas import tpu as pltpu
+from jax.sharding import Mesh
 from jax.sharding import PartitionSpec as P
 
 HEADS = 16
 LATENT = 512
+NOPE = 128
 SLABS_REQ = 16
 LANES = 128
 CHUNKS = LATENT // LANES
 MSG = 8
+CORES = 2
 
 score_scale = 192.0 ** (-0.5)
 neg_fill = -1e30
@@ -35,21 +38,29 @@
     return jnp.sum(jnp.where(iota(rows.shape, 0) == at, rows, 0.0), axis=0, keepdims=True)
 
 
-def prep_kernel(nope_ref, rope_ref, out_ref):
-    nope = nope_ref[0, :1].astype(f32)
-    rope = rope_ref[0, :1].astype(f32)
-    rope = jnp.concatenate([rope, jnp.zeros((1, LANES - rope.shape[1]), f32)], axis=1)
+def prep_kernel(idx_ref, query_ref, far_nope_ref, far_rope_ref, out_ref):
+    first = idx_ref[0] % CORES == 0
+
+    def padded(row):
+        row = row.astype(f32)
+        return jnp.concatenate([row, jnp.zeros((1, LANES - row.shape[1]), f32)], axis=1)
+
+    own = query_ref[0, :1, :NOPE].astype(f32), padded(query_ref[0, :1, NOPE:])
+    far = far_nope_ref[0, :1].astype(f32), padded(far_rope_ref[0, :1])
     shape = (out_ref.shape[0], LANES)
-    pair = jnp.where(iota(shape, 0) % 2 == 0, nope, rope)
-    out_ref[...] = pair.astype(bf16)
+    line = iota(shape, 0) % (2 * CORES)
+    near = (line < 2) == first
+    rows = jnp.where(
+        near, jnp.where(line % 2 == 0, own[0], own[1]), jnp.where(line % 2 == 0, far[0], far[1])
+    )
+    out_ref[...] = rows.astype(bf16)
 
 
 def attend_kernel(
     idx_ref,
     lengths_ref,
     got_ref,
-    nope_ref,
-    rope_ref,
+    query_ref,
     w_uk_ref,
     w_uv_ref,
     newlat_ref,
@@ -75,7 +86,7 @@
     want = (req_v * HEADS + part % HEADS) * 2 + part // HEADS
     pick = jnp.where(iota((2 * HEADS, rows), 1) == want, 1.0, 0.0).astype(bf16)
     q_all = nn_dot(pick, got_ref[...]).astype(bf16)
-    rope_dim = rope_ref.shape[-1]
+    rope_dim = query_ref.shape[-1] - NOPE
     q_nope, q_rope = q_all[:HEADS], q_all[HEADS:, :rope_dim]
 
     wide = jnp.concatenate([q_nope] * HEADS, axis=1)
@@ -109,7 +120,7 @@
     message = nn_dot(spread, stacked).astype(bf16)
     send_ref[pl.ds(pl.multiple_of(req * (HEADS * MSG), HEADS * MSG), HEADS * MSG), :] = message
 
-    nope, rope = nope_ref[0], rope_ref[0]
+    nope, rope = query_ref[0, :, :NOPE], query_ref[0, :, NOPE:]
     own_lat = nn_dot(nope[:1], w_uk_ref[0, own_head]).astype(bf16).astype(f32)
     newlat = picked_row(newlat_ref[0], own_req)
     own_score = (
@@ -143,17 +154,19 @@
     aux_ref[CHUNKS + 2 :, :] = jnp.zeros((MSG - CHUNKS - 2, LANES), f32)
 
 
-def combine_kernel(idx_ref, map_ref, got_ref, aux_ref, w_uv_ref, out_ref):
+def combine_kernel(idx_ref, map_ref, got_ref, far_ref, aux_ref, w_uv_ref, out_ref):
     holder = idx_ref[0]
     own_req = holder // HEADS
     own_head = holder % HEADS
+    core = holder % CORES
     own = aux_ref[...]
     own_score = own[CHUNKS : CHUNKS + 1]
     messages, levels = [], []
     top = own_score
     for s in range(SLABS_REQ):
         slot = map_ref[0, own_req * SLABS_REQ + s]
-        message = got_ref[pl.ds(pl.multiple_of(slot * MSG, MSG), MSG), :].astype(f32)
+        at = pl.ds(pl.multiple_of(((slot // CORES) * CORES + core) * MSG, MSG), MSG)
+        message = jnp.where(slot % CORES == core, got_ref[at, :], far_ref[at, :]).astype(f32)
         level = message[CHUNKS : CHUNKS + 1] + (
             message[CHUNKS + 1 : CHUNKS + 2] + message[CHUNKS + 2 : CHUNKS + 3]
         )
@@ -183,15 +196,19 @@
         out_shape=out_shape,
         in_specs=in_specs,
         out_specs=(VMEM,) * len(out_shape) if many else VMEM,
-        compiler_params=pltpu.CompilerParams(vmem_limit_bytes=12 * 1024 * 1024),
+        compiler_params=pltpu.CompilerParams(vmem_limit_bytes=12 << 20),
         cost_estimate=pl.CostEstimate(flops=flops, bytes_accessed=1 << 20, transcendentals=0),
     )
 
 
-def exchanged(rows, per_device):
-    holders = lax.axis_size("holders")
-    tiles = rows.reshape(holders, per_device, LANES)
-    return lax.all_to_all(tiles, "holders", 0, 0, tiled=True).reshape(rows.shape)
+def exchanged(rows, per_chip):
+    chips = lax.axis_size("chips")
+    tiles = rows.reshape(chips, per_chip, LANES)
+    return lax.all_to_all(tiles, "chips", 0, 0, tiled=True).reshape(rows.shape)
+
+
+def swapped(x):
+    return lax.ppermute(x, "cores", [(k, (k + 1) % CORES) for k in range(CORES)])
 
 
 def shards(
@@ -207,27 +224,28 @@
     deep_positions,
     lengths,
 ):
-    holders = lax.axis_size("holders")
-    holder = lax.axis_index("holders").astype(jnp.int32).reshape(1)
+    chips = lax.axis_size("chips")
+    holder = lax.axis_index("chips") * CORES + lax.axis_index("cores")
+    holder = holder.astype(jnp.int32).reshape(1)
     shape = jax.ShapeDtypeStruct
     q_nope, q_rope = q_nope.swapaxes(0, 1), q_rope.swapaxes(0, 1)
     shallow_cache, deep_cache = shallow_cache.swapaxes(2, 3), deep_cache.swapaxes(2, 3)
-    queries = call(prep_kernel, shape((holders * 2, LANES), bf16), [VMEM] * 2, 1 << 33)(
-        q_nope, q_rope
-    )
-    queries, holder = lax.optimization_barrier((queries, holder))
-    queries = exchanged(queries, 2)
+    far_nope, far_rope = swapped(q_nope), swapped(q_rope)
+    query = jnp.concatenate([q_nope, q_rope], axis=-1)
+    queries = call(
+        prep_kernel, shape((chips * CORES * 2, LANES), bf16), [SMEM] + [VMEM] * 3, 1 << 33
+    )(holder, query, far_nope, far_rope)
+    queries = exchanged(queries, CORES * 2)
     partials, aux = call(
         attend_kernel,
-        (shape((holders * MSG, LANES), bf16), shape((MSG, LANES), f32)),
-        [SMEM, SMEM] + [VMEM] * 11,
+        (shape((chips * CORES * MSG, LANES), bf16), shape((MSG, LANES), f32)),
+        [SMEM, SMEM] + [VMEM] * 10,
         1 << 24,
     )(
         holder,
         lengths,
         queries,
-        q_nope,
-        q_rope,
+        query,
         w_uk,
         w_uv,
         new_latent,
@@ -237,15 +255,19 @@
         deep_cache,
         deep_positions,
     )
-    partials = exchanged(partials, MSG)
-    rows = call(combine_kernel, shape(q_nope.shape, bf16), [SMEM, SMEM] + [VMEM] * 3, 1 << 20)(
-        holder, slab_map, partials, aux, w_uv
+    partials = exchanged(partials, CORES * MSG)
+    rows = call(combine_kernel, shape(q_nope.shape, bf16), [SMEM, SMEM] + [VMEM] * 4, 1 << 20)(
+        holder, slab_map, partials, swapped(partials), aux, w_uv
     )
     return rows.swapaxes(0, 1)
 
 
 def solution(mesh):
-    spread = ("groups", "holders")
+    groups, holders = mesh.shape["groups"], mesh.shape["holders"]
+    mesh = Mesh(
+        mesh.devices.reshape(groups, holders // CORES, CORES), ("groups", "chips", "cores")
+    )
+    spread = ("groups", "chips", "cores")
     in_specs = (
         P(None, spread, None),
         P(None, spread, None),

time: 66.6 us -> 63.3 us (0.950)
  blocking collectives: 61.3 us -> 32.8 us
  starting transfers between devices: 0 us -> 23.9 us
  waiting for transfers between devices: 0 us -> 1.78 us
  local copies, waits for them, and re-layouts: 1.35 us -> 0.05 us
  other arithmetic: 0 us -> 0.68 us
    all_to_all x2, blocking collectives: 61.3 us -> 32.8 us  [exchanged(): return lax.all_to_all(tiles, 'chips', 0, 0, tiled=True).reshape(rows.shape)]
    ppermute x0 -> x3, starting transfers between devices: none -> 23.9 us  [swapped(): lax.ppermute(x, 'cores', [(k, (k + 1) % CORES) for k in range(CORES)])]
    ppermute x0 -> x3, waiting for transfers between devices: none -> 1.78 us  [swapped(): lax.ppermute(x, 'cores', [(k, (k + 1) % CORES) for k in range(CORES)])]
    unnamed x22 -> x18, local copies, waits for them, and re-layouts: 1.35 us -> 0.05 us
    concatenate x0 -> x1, other arithmetic: none -> 0.68 us  [shards(): query = jnp.concatenate([q_nope, q_rope], axis=-1)]
  transfers between devices with their start and end apart: 0 -> 3, of which waited for: 0 -> 2; matrix products, arithmetic and copies ran while one was open for 0% -> 1% of each run, Pallas kernels for 0% -> 0%
where the time goes in v2:
time: 63.3 us; the launch traced here: 63.1 us
  blocking collectives  32.8 us (52%)
  starting transfers between devices  23.9 us (38%)
  Pallas kernels  3.84 us (6%)
  waiting for transfers between devices  1.78 us (3%)
  other arithmetic  0.68 us (1%)
    all_to_all x2, blocking collectives, exchanged(): return lax.all_to_all(tiles, 'chips', 0, 0, tiled=True).reshape(rows.shape)  32.8 us
    ppermute x3, starting transfers between devices, swapped(): lax.ppermute(x, 'cores', [(k, (k + 1) % CORES) for k in range(CORES)])  23.9 us
    pallas_call x1, Pallas kernels, shards(): call(attend_kernel, (shape((chips * CORES * MSG, LANES), bf16), shape((MS...  2.44 us
    ppermute x3, waiting for transfers between devices, swapped(): lax.ppermute(x, 'cores', [(k, (k + 1) % CORES) for k in range(CORES)])  1.78 us
    pallas_call x1, Pallas kernels, shards(): call(combine_kernel, shape(q_nope.shape, bf16), [SMEM, SMEM] + [VMEM] * 4...  1.35 us
  transfers between devices with their start and end apart: 3, of which 2 were waited for; matrix products, arithmetic and copies ran while one was open for 1% of the time, Pallas kernels for 0%

profile of v2, /device:TPU:513, one launch (start us, length us, event | category | flops | bytes accessed | tf_op | source)
XLA Modules:
  0.0 63.1 jit_solution(4239331824935871250)
XLA Ops:
  0.0 20.4 %collective-permute-start = (bf16[1,2,128]{2,1,0:T(2,128)(2,1)}, bf16[1,2,128]{2,1,0:T(2,128)(2,1)S(1)}, u32[]{:S(2)}, u32[]{:S(2)}) collective-permute-start(bf16[1,2,128]{2,1,0:T(2,128)(2,1)} %bitcast.19), channel_id=1, source_target_pairs={{0,1},{1,0},{2,3},{3,2},{4,5},{5,4},{6,7},{7,6},{8,9},{9,8},{10,11... | collective-permute-start | bytes 1544 | tf_op jit(solution)/shard_map/ppermute | solution.py:211
  20.4 0.0 collective-permute-start.1
  20.4 0.7 %pad_maximum_fusion.query_ref = bf16[1,2,192]{2,1,0:T(2,128)(2,1)S(1)} fusion(bf16[1,2,64]{2,1,0:T(2,128)(2,1)} %bitcast.18, bf16[1,2,128]{2,1,0:T(2,128)(2,1)} %bitcast.20), kind=kLoop, calls=%fused_computation | loop fusion | flops 1536 | bytes 1536 | tf_op jit(solution)/shard_map/concatenate | solution.py:234
  21.1 0.6 collective-permute-done.1.far_rope_ref
  21.7 0.0 collective-permute-done.far_nope_ref
  21.7 0.0 copy-start
  21.7 0.0 copy-start.1
  21.7 0.0 copy-start.2
  21.7 0.0 copy-start.3
  21.7 0.0 copy-start.4
  21.7 0.0 copy-start.5
  21.8 0.0 copy-start.6
  21.8 0.0 copy-start.7
  21.8 0.0 copy-start.8
  21.9 16.1 %all_to_all.10 = bf16[64,4,128]{2,1,0:T(4,128)(2,1)S(1)} all-to-all(bf16[64,4,128]{2,1,0:T(4,128)(2,1)S(1)} %bitcast.16), channel_id=1, replica_groups=mesh['groups'=2,'chips'=64,'cores'=2] {'chips'}, dimensions={0} | all-to-all | bytes 131072 | tf_op jit(solution)/shard_map/all_to_all | solution.py:207
  38.0 0.0 copy-done
  38.0 0.0 copy-done.1
  38.0 0.0 copy-done.2
  38.0 0.0 copy-done.3
  38.0 0.0 copy-done.4
  38.0 0.0 copy-done.5
  38.0 0.0 copy-done.6
  38.0 0.0 copy-done.7
  38.0 0.0 copy-done.8
  38.0 2.4 %shard_map.110 = (bf16[1024,128]{1,0:T(8,128)(2,1)S(1)}, f32[8,128]{1,0:T(8,128)S(1)}) custom-call(s32[1]{0:T(128)} %bitcast.idx_ref, s32[8]{0:T(128)S(1)} %copy-done.8, bf16[256,128]{1,0:T(8,128)(2,1)S(1)} %bitcast.14, bf16[1,2,192]{2,1,0:T(2,128)(2,1)S(1)} %pad_maximum_fusion.query_ref, bf16[2,16,128,512]{3,2,1,0:T(8,128)(2,1)S(1)} %copy-done.1, ...), custom_call_target="tpu_custom_call" | custom-call | flops 16777216 | bytes 1048576 | tf_op jit(solution)/shard_map/pallas_call | solution.py:239
  40.5 16.7 %all_to_all.11 = bf16[64,16,128]{2,1,0:T(8,128)(2,1)S(1)} all-to-all(bf16[64,16,128]{2,1,0:T(8,128)(2,1)S(1)} %bitcast.15), channel_id=1, replica_groups=mesh['groups'=2,'chips'=64,'cores'=2] {'chips'}, dimensions={0} | all-to-all | bytes 524288 | tf_op jit(solution)/shard_map/all_to_all | solution.py:207
  57.2 3.5 %collective-permute-start.2 = (bf16[1024,128]{1,0:T(8,128)(2,1)S(1)}, bf16[1024,128]{1,0:T(8,128)(2,1)S(1)}, u32[]{:S(2)}, u32[]{:S(2)}) collective-permute-start(bf16[1024,128]{1,0:T(8,128)(2,1)S(1)} %bitcast.11), channel_id=1, source_target_pairs={{0,1},{1,0},{2,3},{3,2},{4,5},{5,4},{6,7},{7,6},{8,9},{9,8},{10,11... | collective-permute-start | bytes 786440 | tf_op jit(solution)/shard_map/ppermute | solution.py:211
  60.6 1.2 %collective-permute-done.2.far_ref = bf16[1024,128]{1,0:T(8,128)(2,1)S(1)} collective-permute-done((bf16[1024,128]{1,0:T(8,128)(2,1)S(1)}, bf16[1024,128]{1,0:T(8,128)(2,1)S(1)}, u32[]{:S(2)}, u32[]{:S(2)}) %collective-permute-start.2) | collective-permute-done | bytes 262176 | tf_op jit(solution)/shard_map/ppermute | solution.py:211
  61.8 1.4 %shard_map.111 = bf16[1,2,128]{2,1,0:T(2,128)(2,1)} custom-call(s32[1]{0:T(128)} %bitcast.idx_ref, s32[1,128]{1,0:T(1,128)S(1)} %copy-done.6, bf16[1024,128]{1,0:T(8,128)(2,1)S(1)} %bitcast.12, bf16[1024,128]{1,0:T(8,128)(2,1)S(1)} %collective-permute-done.2.far_ref, f32[8,128]{1,0:T(8,128)S(1)} %get-tuple-element.8.aux_ref, ...), custom_call_target="tpu_custom_call" | custom-call | flops 1048576 | bytes 1048576 | tf_op jit(solution)/shard_map/pallas_call | solution.py:259
  (1 shorter events, 0.0 us)
Async XLA Ops:
  0.0 21.7 %collective-permute-start = (bf16[1,2,128]{2,1,0:T(2,128)(2,1)}, bf16[1,2,128]{2,1,0:T(2,128)(2,1)S(1)}, u32[]{:S(2)}, u32[]{:S(2)}) collective-permute-start(bf16[1,2,128]{2,1,0:T(2,128)(2,1)} %bitcast.19), channel_id=1, source_target_pairs={{0,1},{1,0},{2,3},{3,2},{4,5},{5,4},{6,7},{7,6},{8,9},{9,8},{10,11... | collective-permute-start | bytes 1544 | tf_op jit(solution)/shard_map/ppermute | solution.py:211
  20.4 1.3 %collective-permute-start.1 = (bf16[1,2,64]{2,1,0:T(2,128)(2,1)}, bf16[1,2,64]{2,1,0:T(2,128)(2,1)S(1)}, u32[]{:S(2)}, u32[]{:S(2)}) collective-permute-start(bf16[1,2,64]{2,1,0:T(2,128)(2,1)} %bitcast.17), channel_id=1, source_target_pairs={{0,1},{1,0},{2,3},{3,2},{4,5},{5,4},{6,7},{7,6},{8,9},{9,8},{10,11... | collective-permute-start | bytes 776 | tf_op jit(solution)/shard_map/ppermute | solution.py:211
  21.7 16.2 %copy-start = (bf16[2,16,512,128]{3,2,1,0:T(8,128)(2,1)S(1)}, bf16[2,16,512,128]{3,2,1,0:T(8,128)(2,1)}, u32[]{:S(2)}) copy-start(bf16[2,16,512,128]{3,2,1,0:T(8,128)(2,1)} %w_uv_ref.3) | copy-start | bytes 12582916
  21.7 16.2 %copy-start.1 = (bf16[2,16,128,512]{3,2,1,0:T(8,128)(2,1)S(1)}, bf16[2,16,128,512]{3,2,1,0:T(8,128)(2,1)}, u32[]{:S(2)}) copy-start(bf16[2,16,128,512]{3,2,1,0:T(8,128)(2,1)} %w_uk_ref.1) | copy-start | bytes 12582916
  21.7 16.2 %copy-start.2 = (bf16[1,8,256,576]{2,3,1,0:T(8,128)(2,1)S(1)}, bf16[1,8,256,576]{2,3,1,0:T(8,128)(2,1)}, u32[]{:S(2)}) copy-start(bf16[1,8,256,576]{2,3,1,0:T(8,128)(2,1)} %param.19) | copy-start | bytes 7077892
  21.7 16.2 %copy-start.3 = (bf16[1,1,512,576]{2,3,1,0:T(8,128)(2,1)S(1)}, bf16[1,1,512,576]{2,3,1,0:T(8,128)(2,1)}, u32[]{:S(2)}) copy-start(bf16[1,1,512,576]{2,3,1,0:T(8,128)(2,1)} %param.16) | copy-start | bytes 1769476
  21.7 16.2 %copy-start.4 = (bf16[2,8,576]{2,1,0:T(8,128)(2,1)S(1)}, bf16[2,8,576]{2,1,0:T(8,128)(2,1)}, u32[]{:S(2)}) copy-start(bf16[2,8,576]{2,1,0:T(8,128)(2,1)} %newlat_ref.1) | copy-start | bytes 55300
  21.7 16.2 %copy-start.5 = (s32[1,8,256]{2,1,0:T(8,128)S(1)}, s32[1,8,256]{2,1,0:T(8,128)}, u32[]{:S(2)}) copy-start(s32[1,8,256]{2,1,0:T(8,128)} %deep_pos_ref.1) | copy-start | bytes 24580
  21.8 16.2 %copy-start.6 = (s32[1,128]{1,0:T(1,128)S(1)}, s32[1,128]{1,0:T(1,128)}, u32[]{:S(2)}) copy-start(s32[1,128]{1,0:T(1,128)} %map_ref.3) | copy-start | bytes 1540
  21.8 16.2 %copy-start.7 = (s32[1,1,512]{2,1,0:T(1,128)S(1)}, s32[1,1,512]{2,1,0:T(1,128)}, u32[]{:S(2)}) copy-start(s32[1,1,512]{2,1,0:T(1,128)} %slab_pos_ref.1) | copy-start | bytes 6148
  21.8 16.2 %copy-start.8 = (s32[8]{0:T(128)S(1)}, s32[8]{0:T(128)}, u32[]{:S(2)}) copy-start(s32[8]{0:T(128)} %lengths_ref.1) | copy-start | bytes 100
  57.2 4.6 %collective-permute-start.2 = (bf16[1024,128]{1,0:T(8,128)(2,1)S(1)}, bf16[1024,128]{1,0:T(8,128)(2,1)S(1)}, u32[]{:S(2)}, u32[]{:S(2)}) collective-permute-start(bf16[1024,128]{1,0:T(8,128)(2,1)S(1)} %bitcast.11), channel_id=1, source_target_pairs={{0,1},{1,0},{2,3},{3,2},{4,5},{5,4},{6,7},{7,6},{8,9},{9,8},{10,11... | collective-permute-start | bytes 786440 | tf_op jit(solution)/shard_map/ppermute | solution.py:211

commit v3 on v2

--- a/solution.py
+++ b/solution.py
@@ -1,3 +1,5 @@
+import math
+
 import jax
 import jax.numpy as jnp
 from jax import lax
@@ -14,6 +16,7 @@
 CHUNKS = LATENT // LANES
 MSG = 8
 CORES = 2
+LOG_2 = math.log(2.0)
 
 score_scale = 192.0 ** (-0.5)
 neg_fill = -1e30
@@ -36,6 +39,19 @@
 def picked_row(rows, at):
     rows = rows.astype(f32)
     return jnp.sum(jnp.where(iota(rows.shape, 0) == at, rows, 0.0), axis=0, keepdims=True)
+
+
+def pieces(x):
+    out = []
+    for _ in range(3):
+        out.append(x.astype(bf16))
+        x = x - out[-1].astype(f32)
+    return out
+
+
+def message_level(message):
+    rows = [message[..., CHUNKS + j : CHUNKS + j + 1, :] for j in range(3)]
+    return rows[0] + (rows[1] + rows[2])
 
 
 def prep_kernel(idx_ref, query_ref, far_nope_ref, far_rope_ref, out_ref):
@@ -56,41 +72,38 @@
     out_ref[...] = rows.astype(bf16)
 
 
+def slab_request(map_ref, slot):
+    owners = map_ref[...]
+    place = iota(owners.shape, 1) // SLABS_REQ
+    return jnp.sum(jnp.where(owners == slot, place, 0), axis=1, keepdims=True)
+
+
 def attend_kernel(
     idx_ref,
     lengths_ref,
     got_ref,
-    query_ref,
     w_uk_ref,
-    w_uv_ref,
-    newlat_ref,
     slab_ref,
     slab_pos_ref,
     map_ref,
-    deep_ref,
-    deep_pos_ref,
-    send_ref,
-    aux_ref,
+    keep_ref,
+    give_ref,
 ):
     holder = idx_ref[0]
-    own_req = holder // HEADS
-    own_head = holder % HEADS
-
-    owners = map_ref[...]
-    place = iota(owners.shape, 1) // SLABS_REQ
-    req_v = jnp.sum(jnp.where(owners == holder, place, 0), axis=1, keepdims=True)
+    core = holder % CORES
+    req_v = slab_request(map_ref, holder)
     req = jnp.sum(req_v)
 
-    rows = got_ref.shape[0]
-    part = iota((2 * HEADS, rows), 0)
+    shape = (2 * HEADS, got_ref.shape[0])
+    part = iota(shape, 0)
     want = (req_v * HEADS + part % HEADS) * 2 + part // HEADS
-    pick = jnp.where(iota((2 * HEADS, rows), 1) == want, 1.0, 0.0).astype(bf16)
+    pick = jnp.where(iota(shape, 1) == want, 1.0, 0.0).astype(bf16)
     q_all = nn_dot(pick, got_ref[...]).astype(bf16)
-    rope_dim = query_ref.shape[-1] - NOPE
+    rope_dim = slab_ref.shape[2] - LATENT
     q_nope, q_rope = q_all[:HEADS], q_all[HEADS:, :rope_dim]
 
     wide = jnp.concatenate([q_nope] * HEADS, axis=1)
-    diagonal = iota(wide.shape, 1) // q_nope.shape[1] == iota(wide.shape, 0)
+    diagonal = iota(wide.shape, 1) // NOPE == iota(wide.shape, 0)
     wide = jnp.where(diagonal, wide, jnp.zeros_like(wide))
     w_uk = w_uk_ref[0].reshape(wide.shape[1], LATENT)
     q_lat = nn_dot(wide, w_uk).astype(bf16)
@@ -107,20 +120,37 @@
     level = jnp.where(total > 0.0, top + jnp.log(safe), neg_fill)
 
     blocks = [out[:, j * LANES : (j + 1) * LANES].astype(bf16) for j in range(CHUNKS)]
-    rest = jnp.broadcast_to(level, (HEADS, LANES))
-    for _ in range(3):
-        piece = rest.astype(bf16)
-        blocks.append(piece)
-        rest = rest - piece.astype(f32)
+    blocks += pieces(jnp.broadcast_to(level, (HEADS, LANES)))
     stacked = jnp.concatenate(blocks, axis=0)
     shape = (HEADS * MSG, stacked.shape[0])
     line, column = iota(shape, 0), iota(shape, 1)
-    place = (line % MSG) * HEADS + line // MSG
-    spread = jnp.where((column == place) & (line % MSG < len(blocks)), 1.0, 0.0).astype(bf16)
+    half = HEADS // CORES * MSG
+    parity = jnp.where(line < half, core, 1 - core)
+    head = line % half // MSG * CORES + parity
+    wanted = (column == line % MSG * HEADS + head) & (line % MSG < len(blocks))
+    spread = jnp.where(wanted, 1.0, 0.0).astype(bf16)
     message = nn_dot(spread, stacked).astype(bf16)
-    send_ref[pl.ds(pl.multiple_of(req * (HEADS * MSG), HEADS * MSG), HEADS * MSG), :] = message
-
+    keep_ref[...] = message[:half]
+    give_ref[...] = message[half:]
+
+
+def own_kernel(
+    idx_ref,
+    lengths_ref,
+    query_ref,
+    w_uk_ref,
+    w_uv_ref,
+    newlat_ref,
+    map_ref,
+    deep_ref,
+    deep_pos_ref,
+    aux_ref,
+):
+    holder = idx_ref[0]
+    own_req = holder // HEADS
+    own_head = holder % HEADS
     nope, rope = query_ref[0, :, :NOPE], query_ref[0, :, NOPE:]
+
     own_lat = nn_dot(nope[:1], w_uk_ref[0, own_head]).astype(bf16).astype(f32)
     newlat = picked_row(newlat_ref[0], own_req)
     own_score = (
@@ -151,25 +181,46 @@
     total = own_factor + block_sum * far_factor
     mixed = ((own_factor * newlat[:, :LATENT] + block_out * far_factor) / total).astype(bf16)
     aux_ref[CHUNKS + 1 : CHUNKS + 2, :] = nn_dot(mixed, w_uv_ref[1, own_head])
-    aux_ref[CHUNKS + 2 :, :] = jnp.zeros((MSG - CHUNKS - 2, LANES), f32)
-
-
-def combine_kernel(idx_ref, map_ref, got_ref, far_ref, aux_ref, w_uv_ref, out_ref):
+
+    for row, slot in ((CHUNKS + 2, holder), (CHUNKS + 3, holder + 1 - 2 * (holder % CORES))):
+        req = slab_request(map_ref, slot).astype(f32)
+        aux_ref[row : row + 1, :] = jnp.broadcast_to(req, (1, LANES))
+
+
+def merge_kernel(keep_ref, far_ref, aux_ref, send_ref):
+    near_req, far_req = aux_ref[CHUNKS + 2 : CHUNKS + 3, :], aux_ref[CHUNKS + 3 : CHUNKS + 4, :]
+    blocks = keep_ref.shape[0] // MSG
+    near = keep_ref[...].astype(f32).reshape(blocks, MSG, LANES)
+    far = far_ref[...].astype(f32).reshape(blocks, MSG, LANES)
+    near_level, far_level = message_level(near), message_level(far)
+    top = jnp.maximum(near_level, far_level)
+    near_factor, far_factor = jnp.exp(near_level - top), jnp.exp(far_level - top)
+    total = near_factor + far_factor
+    merged = (near_factor * near + far_factor * far) / total
+    level = top + (jnp.log(total) - LOG_2)
+    line = iota(merged.shape, 1)
+    for j, piece in enumerate(pieces(level)):
+        merged = jnp.where(line == CHUNKS + j, piece.astype(f32), merged)
+    same = near_req == far_req
+    near = jnp.where(same, merged, near).reshape(keep_ref.shape)
+    far = jnp.where(same, merged, far).reshape(keep_ref.shape)
+    rows = keep_ref.shape[0]
+    for b in range(send_ref.shape[0] // rows):
+        send_ref[b * rows : (b + 1) * rows, :] = jnp.where(near_req == b, near, far).astype(bf16)
+
+
+def combine_kernel(idx_ref, map_ref, got_ref, aux_ref, w_uv_ref, out_ref):
     holder = idx_ref[0]
     own_req = holder // HEADS
     own_head = holder % HEADS
-    core = holder % CORES
     own = aux_ref[...]
     own_score = own[CHUNKS : CHUNKS + 1]
     messages, levels = [], []
     top = own_score
     for s in range(SLABS_REQ):
-        slot = map_ref[0, own_req * SLABS_REQ + s]
-        at = pl.ds(pl.multiple_of(((slot // CORES) * CORES + core) * MSG, MSG), MSG)
-        message = jnp.where(slot % CORES == core, got_ref[at, :], far_ref[at, :]).astype(f32)
-        level = message[CHUNKS : CHUNKS + 1] + (
-            message[CHUNKS + 1 : CHUNKS + 2] + message[CHUNKS + 2 : CHUNKS + 3]
-        )
+        chip = map_ref[0, own_req * SLABS_REQ + s] // CORES
+        message = got_ref[pl.ds(pl.multiple_of(chip * MSG, MSG), MSG), :].astype(f32)
+        level = message_level(message)
         messages.append(message)
         levels.append(level)
         top = jnp.maximum(top, level)
@@ -236,28 +287,20 @@
         prep_kernel, shape((chips * CORES * 2, LANES), bf16), [SMEM] + [VMEM] * 3, 1 << 33
     )(holder, query, far_nope, far_rope)
     queries = exchanged(queries, CORES * 2)
-    partials, aux = call(
-        attend_kernel,
-        (shape((chips * CORES * MSG, LANES), bf16), shape((MSG, LANES), f32)),
-        [SMEM, SMEM] + [VMEM] * 10,
-        1 << 24,
-    )(
-        holder,
-        lengths,
-        queries,
-        query,
-        w_uk,
-        w_uv,
-        new_latent,
-        shallow_cache,
-        slot_positions,
-        slab_map,
-        deep_cache,
-        deep_positions,
-    )
-    partials = exchanged(partials, CORES * MSG)
-    rows = call(combine_kernel, shape(q_nope.shape, bf16), [SMEM, SMEM] + [VMEM] * 4, 1 << 20)(
-        holder, slab_map, partials, swapped(partials), aux, w_uv
+    block = shape((HEADS // CORES * MSG, LANES), bf16)
+    keep, give = call(attend_kernel, (block, block), [SMEM, SMEM] + [VMEM] * 5, 1 << 24)(
+        holder, lengths, queries, w_uk, shallow_cache, slot_positions, slab_map
+    )
+    far = swapped(give)
+    aux = call(own_kernel, shape((MSG, LANES), f32), [SMEM, SMEM] + [VMEM] * 7, 1 << 24)(
+        holder, lengths, query, w_uk, w_uv, new_latent, slab_map, deep_cache, deep_positions
+    )
+    partials = call(merge_kernel, shape((chips * MSG, LANES), bf16), [VMEM] * 3, 1 << 20)(
+        keep, far, aux
+    )
+    partials = exchanged(partials, MSG)
+    rows = call(combine_kernel, shape(q_nope.shape, bf16), [SMEM, SMEM] + [VMEM] * 3, 1 << 20)(
+        holder, slab_map, partials, aux, w_uv
     )
     return rows.swapaxes(0, 1)
 

time: 63.3 us -> 60.3 us (0.953)
  starting transfers between devices: 23.9 us -> 21.9 us
  waiting for transfers between devices: 1.78 us -> 0.62 us
  Pallas kernels: 3.84 us -> 4.49 us
    ppermute x3, starting transfers between devices: 23.9 us -> 21.9 us  [swapped(): lax.ppermute(x, 'cores', [(k, (k + 1) % CORES) for k in range(CORES)])]
    ppermute x3, waiting for transfers between devices: 1.78 us -> 0.62 us  [swapped(): lax.ppermute(x, 'cores', [(k, (k + 1) % CORES) for k in range(CORES)])]
    pallas_call x2 -> x4, Pallas kernels: 3.8 us -> 4.45 us  [the longest x1 1.8 us: shards(): call(attend_kernel, (block, block), [SMEM, SMEM] + [VMEM] * 5, 1 << 24)]
  transfers between devices with their start and end apart: 3 -> 3, of which waited for: 2 -> 1; matrix products, arithmetic and copies ran while one was open for 1% -> 1% of each run, Pallas kernels for 0% -> 2%
where the time goes in v3:
time: 60.3 us; the launch traced here: 60.1 us
  blocking collectives  32.3 us (54%)
  starting transfers between devices  21.9 us (36%)
  Pallas kernels  4.49 us (7%)
  other arithmetic  0.68 us (1%)
  waiting for transfers between devices  0.62 us (1%)
    all_to_all x2, blocking collectives, exchanged(): return lax.all_to_all(tiles, 'chips', 0, 0, tiled=True).reshape(rows.shape)  32.3 us
    ppermute x3, starting transfers between devices, swapped(): lax.ppermute(x, 'cores', [(k, (k + 1) % CORES) for k in range(CORES)])  21.9 us
    pallas_call x1, Pallas kernels, shards(): call(attend_kernel, (block, block), [SMEM, SMEM] + [VMEM] * 5, 1 << 24)  1.8 us
    pallas_call x1, Pallas kernels, shards(): call(combine_kernel, shape(q_nope.shape, bf16), [SMEM, SMEM] + [VMEM] * 3...  1.31 us
    pallas_call x1, Pallas kernels, shards(): call(own_kernel, shape((MSG, LANES), f32), [SMEM, SMEM] + [VMEM] * 7, 1 <...  1.25 us
  transfers between devices with their start and end apart: 3, of which 1 were waited for; matrix products, arithmetic and copies ran while one was open for 1% of the time, Pallas kernels for 2%

profile of v3, /device:TPU:513, one launch (start us, length us, event | category | flops | bytes accessed | tf_op | source)
XLA Modules:
  0.0 60.1 jit_solution(15274134261220922660)
XLA Ops:
  0.0 20.4 %collective-permute-start = (bf16[1,2,128]{2,1,0:T(2,128)(2,1)}, bf16[1,2,128]{2,1,0:T(2,128)(2,1)S(1)}, u32[]{:S(2)}, u32[]{:S(2)}) collective-permute-start(bf16[1,2,128]{2,1,0:T(2,128)(2,1)} %bitcast.18), channel_id=1, source_target_pairs={{0,1},{1,0},{2,3},{3,2},{4,5},{5,4},{6,7},{7,6},{8,9},{9,8},{10,11... | collective-permute-start | bytes 1544 | tf_op jit(solution)/shard_map/ppermute | solution.py:262
  20.4 0.0 collective-permute-start.1
  20.4 0.7 %pad_maximum_fusion.query_ref = bf16[1,2,192]{2,1,0:T(2,128)(2,1)S(1)} fusion(bf16[1,2,64]{2,1,0:T(2,128)(2,1)} %bitcast.17, bf16[1,2,128]{2,1,0:T(2,128)(2,1)} %bitcast.19), kind=kLoop, calls=%fused_computation | loop fusion | flops 1536 | bytes 1536 | tf_op jit(solution)/shard_map/concatenate | solution.py:285
  21.1 0.6 %collective-permute-done.1.far_rope_ref = bf16[1,2,64]{2,1,0:T(2,128)(2,1)S(1)} collective-permute-done((bf16[1,2,64]{2,1,0:T(2,128)(2,1)}, bf16[1,2,64]{2,1,0:T(2,128)(2,1)S(1)}, u32[]{:S(2)}, u32[]{:S(2)}) %collective-permute-start.1) | collective-permute-done | bytes 288 | tf_op jit(solution)/shard_map/ppermute | solution.py:262
  21.7 0.0 collective-permute-done.far_nope_ref
  21.7 0.0 copy-start
  21.7 0.0 copy-start.3
  21.7 0.0 copy-start.6
  21.7 0.0 copy-start.7
  21.7 0.0 copy-start.8
  21.7 0.0 copy-start.2
  21.8 0.0 copy-start.1
  21.8 0.0 copy-start.4
  21.8 0.0 copy-start.5
  21.9 16.1 %all_to_all.10 = bf16[64,4,128]{2,1,0:T(4,128)(2,1)S(1)} all-to-all(bf16[64,4,128]{2,1,0:T(4,128)(2,1)S(1)} %bitcast.15), channel_id=1, replica_groups=mesh['groups'=2,'chips'=64,'cores'=2] {'chips'}, dimensions={0} | all-to-all | bytes 131072 | tf_op jit(solution)/shard_map/all_to_all | solution.py:258
  38.0 0.0 copy-done
  38.0 0.0 copy-done.3
  38.0 0.0 copy-done.6
  38.0 0.0 copy-done.7
  38.0 0.0 copy-done.8
  38.0 1.8 %shard_map.110 = (bf16[64,128]{1,0:T(8,128)(2,1)S(1)}, bf16[64,128]{1,0:T(8,128)(2,1)S(1)}) custom-call(s32[1]{0:T(128)} %bitcast.idx_ref, s32[8]{0:T(128)S(1)} %copy-done.8, bf16[256,128]{1,0:T(8,128)(2,1)S(1)} %bitcast.14, bf16[2,16,128,512]{3,2,1,0:T(8,128)(2,1)S(1)} %copy-done, bf16[1,1,576,512]{3,2,1,0:T(8,128)(2,1)S(1)} %bitcast.11, ...), custom_call_target="tpu_custom_call" | custom-call | flops 16777216 | bytes 1048576 | tf_op jit(solution)/shard_map/pallas_call | solution.py:291
  39.8 1.5 %collective-permute-start.2 = (bf16[64,128]{1,0:T(8,128)(2,1)S(1)}, bf16[64,128]{1,0:T(8,128)(2,1)S(1)}, u32[]{:S(2)}, u32[]{:S(2)}) collective-permute-start(bf16[64,128]{1,0:T(8,128)(2,1)S(1)} %get-tuple-element.8), channel_id=1, source_target_pairs={{0,1},{1,0},{2,3},{3,2},{4,5},{5,4},{6,7},{7,6},{8,9},{9,8},{10,11... | collective-permute-start | bytes 49160 | tf_op jit(solution)/shard_map/ppermute | solution.py:262
  41.3 0.0 copy-done.2
  41.3 0.0 copy-done.1
  41.3 0.0 copy-done.4
  41.3 0.0 copy-done.5
  41.3 1.2 %shard_map.111.aux_ref = f32[8,128]{1,0:T(8,128)S(1)} custom-call(s32[1]{0:T(128)} %bitcast.idx_ref, s32[8]{0:T(128)S(1)} %copy-done.8, bf16[1,2,192]{2,1,0:T(2,128)(2,1)S(1)} %pad_maximum_fusion.query_ref, bf16[2,16,128,512]{3,2,1,0:T(8,128)(2,1)S(1)} %copy-done, bf16[2,16,512,128]{3,2,1,0:T(8,128)(2,1)S(1)} %copy-done.1, bf16[2,8,576]{2,1,0:T(8,128)(2,1)S(1)} %copy-done.4, ...), custom_call_target="tpu_custom_call" | custom-call | flops 16777216 | bytes 1048576 | tf_op jit(solution)/shard_map/pallas_call | solution.py:295
  42.5 0.0 collective-permute-done.2.far_ref
  42.6 0.1 shard_map.112
  42.6 16.2 %all_to_all.11 = bf16[64,8,128]{2,1,0:T(8,128)(2,1)S(1)} all-to-all(bf16[64,8,128]{2,1,0:T(8,128)(2,1)S(1)} %bitcast.13), channel_id=1, replica_groups=mesh['groups'=2,'chips'=64,'cores'=2] {'chips'}, dimensions={0} | all-to-all | bytes 262144 | tf_op jit(solution)/shard_map/all_to_all | solution.py:258
  58.8 1.3 %shard_map.113 = bf16[1,2,128]{2,1,0:T(2,128)(2,1)} custom-call(s32[1]{0:T(128)} %bitcast.idx_ref, s32[1,128]{1,0:T(1,128)S(1)} %copy-done.6, bf16[512,128]{1,0:T(8,128)(2,1)S(1)} %bitcast.12, f32[8,128]{1,0:T(8,128)S(1)} %shard_map.111.aux_ref, bf16[2,16,512,128]{3,2,1,0:T(8,128)(2,1)S(1)} %copy-done.1), custom_call_target="tpu_custom_call" | custom-call | flops 1048576 | bytes 1048576 | tf_op jit(solution)/shard_map/pallas_call | solution.py:302
  (1 shorter events, 0.0 us)
Async XLA Ops:
  0.0 21.7 %collective-permute-start = (bf16[1,2,128]{2,1,0:T(2,128)(2,1)}, bf16[1,2,128]{2,1,0:T(2,128)(2,1)S(1)}, u32[]{:S(2)}, u32[]{:S(2)}) collective-permute-start(bf16[1,2,128]{2,1,0:T(2,128)(2,1)} %bitcast.18), channel_id=1, source_target_pairs={{0,1},{1,0},{2,3},{3,2},{4,5},{5,4},{6,7},{7,6},{8,9},{9,8},{10,11... | collective-permute-start | bytes 1544 | tf_op jit(solution)/shard_map/ppermute | solution.py:262
  20.4 1.3 %collective-permute-start.1 = (bf16[1,2,64]{2,1,0:T(2,128)(2,1)}, bf16[1,2,64]{2,1,0:T(2,128)(2,1)S(1)}, u32[]{:S(2)}, u32[]{:S(2)}) collective-permute-start(bf16[1,2,64]{2,1,0:T(2,128)(2,1)} %bitcast.16), channel_id=1, source_target_pairs={{0,1},{1,0},{2,3},{3,2},{4,5},{5,4},{6,7},{7,6},{8,9},{9,8},{10,11... | collective-permute-start | bytes 776 | tf_op jit(solution)/shard_map/ppermute | solution.py:262
  21.7 16.2 %copy-start = (bf16[2,16,128,512]{3,2,1,0:T(8,128)(2,1)S(1)}, bf16[2,16,128,512]{3,2,1,0:T(8,128)(2,1)}, u32[]{:S(2)}) copy-start(bf16[2,16,128,512]{3,2,1,0:T(8,128)(2,1)} %w_uk_ref.3) | copy-start | bytes 12582916
  21.7 16.2 %copy-start.3 = (bf16[1,1,512,576]{2,3,1,0:T(8,128)(2,1)S(1)}, bf16[1,1,512,576]{2,3,1,0:T(8,128)(2,1)}, u32[]{:S(2)}) copy-start(bf16[1,1,512,576]{2,3,1,0:T(8,128)(2,1)} %param.16) | copy-start | bytes 1769476
  21.7 16.2 %copy-start.6 = (s32[1,128]{1,0:T(1,128)S(1)}, s32[1,128]{1,0:T(1,128)}, u32[]{:S(2)}) copy-start(s32[1,128]{1,0:T(1,128)} %map_ref.5) | copy-start | bytes 1540
  21.7 16.2 %copy-start.7 = (s32[1,1,512]{2,1,0:T(1,128)S(1)}, s32[1,1,512]{2,1,0:T(1,128)}, u32[]{:S(2)}) copy-start(s32[1,1,512]{2,1,0:T(1,128)} %slab_pos_ref.1) | copy-start | bytes 6148
  21.7 16.2 %copy-start.8 = (s32[8]{0:T(128)S(1)}, s32[8]{0:T(128)}, u32[]{:S(2)}) copy-start(s32[8]{0:T(128)} %lengths_ref.3) | copy-start | bytes 100
  21.7 19.5 %copy-start.2 = (bf16[1,8,256,576]{2,3,1,0:T(8,128)(2,1)S(1)}, bf16[1,8,256,576]{2,3,1,0:T(8,128)(2,1)}, u32[]{:S(2)}) copy-start(bf16[1,8,256,576]{2,3,1,0:T(8,128)(2,1)} %param.19) | copy-start | bytes 7077892
  21.8 19.5 %copy-start.1 = (bf16[2,16,512,128]{3,2,1,0:T(8,128)(2,1)S(1)}, bf16[2,16,512,128]{3,2,1,0:T(8,128)(2,1)}, u32[]{:S(2)}) copy-start(bf16[2,16,512,128]{3,2,1,0:T(8,128)(2,1)} %w_uv_ref.3) | copy-start | bytes 12582916
  21.8 19.5 %copy-start.4 = (bf16[2,8,576]{2,1,0:T(8,128)(2,1)S(1)}, bf16[2,8,576]{2,1,0:T(8,128)(2,1)}, u32[]{:S(2)}) copy-start(bf16[2,8,576]{2,1,0:T(8,128)(2,1)} %newlat_ref.1) | copy-start | bytes 55300
  21.8 19.5 %copy-start.5 = (s32[1,8,256]{2,1,0:T(8,128)S(1)}, s32[1,8,256]{2,1,0:T(8,128)}, u32[]{:S(2)}) copy-start(s32[1,8,256]{2,1,0:T(8,128)} %deep_pos_ref.1) | copy-start | bytes 24580
  39.8 2.8 %collective-permute-start.2 = (bf16[64,128]{1,0:T(8,128)(2,1)S(1)}, bf16[64,128]{1,0:T(8,128)(2,1)S(1)}, u32[]{:S(2)}, u32[]{:S(2)}) collective-permute-start(bf16[64,128]{1,0:T(8,128)(2,1)S(1)} %get-tuple-element.8), channel_id=1, source_target_pairs={{0,1},{1,0},{2,3},{3,2},{4,5},{5,4},{6,7},{7,6},{8,9},{9,8},{10,11... | collective-permute-start | bytes 49160 | tf_op jit(solution)/shard_map/ppermute | solution.py:262

commit v4 on v3

--- a/solution.py
+++ b/solution.py
@@ -78,6 +78,12 @@
     return jnp.sum(jnp.where(owners == slot, place, 0), axis=1, keepdims=True)
 
 
+def length_of(lengths_ref, req):
+    lengths = lengths_ref[...]
+    mine = jnp.where(iota(lengths.shape, 1) == req, lengths, 0)
+    return jnp.sum(mine, axis=1, keepdims=True)
+
+
 def attend_kernel(
     idx_ref,
     lengths_ref,
@@ -86,13 +92,24 @@
     slab_ref,
     slab_pos_ref,
     map_ref,
+    deep_hbm,
+    w_uv_hbm,
     keep_ref,
     give_ref,
+    deep_ref,
+    w_up_ref,
+    sems,
 ):
     holder = idx_ref[0]
     core = holder % CORES
+    copies = [
+        pltpu.make_async_copy(deep_hbm.at[0, holder // HEADS], deep_ref, sems.at[0]),
+        pltpu.make_async_copy(w_uv_hbm.at[0, holder % HEADS], w_up_ref.at[0], sems.at[1]),
+        pltpu.make_async_copy(w_uv_hbm.at[1, holder % HEADS], w_up_ref.at[1], sems.at[2]),
+    ]
+    for copy in copies:
+        copy.start()
     req_v = slab_request(map_ref, holder)
-    req = jnp.sum(req_v)
 
     shape = (2 * HEADS, got_ref.shape[0])
     part = iota(shape, 0)
@@ -111,7 +128,7 @@
     latent = slab_ref[0, 0, :LATENT]
     rotary = slab_ref[0, 0, LATENT:]
     score = (nn_dot(q_lat, latent) + nn_dot(q_rope, rotary)) * score_scale
-    live = slab_pos_ref[0] < lengths_ref[req]
+    live = slab_pos_ref[0] < length_of(lengths_ref, req_v)
     top = jnp.max(jnp.where(live, score, neg_fill), axis=1, keepdims=True)
     weight = jnp.where(live, jnp.exp(jnp.where(live, score - top, 0.0)), 0.0).astype(bf16)
     total = jnp.sum(weight.astype(f32), axis=1, keepdims=True)
@@ -132,6 +149,8 @@
     message = nn_dot(spread, stacked).astype(bf16)
     keep_ref[...] = message[:half]
     give_ref[...] = message[half:]
+    for copy in copies:
+        copy.wait()
 
 
 def own_kernel(
@@ -139,12 +158,13 @@
     lengths_ref,
     query_ref,
     w_uk_ref,
-    w_uv_ref,
+    w_up_ref,
     newlat_ref,
     map_ref,
     deep_ref,
     deep_pos_ref,
     aux_ref,
+    chips_ref,
 ):
     holder = idx_ref[0]
     own_req = holder // HEADS
@@ -162,10 +182,10 @@
     aux_ref[CHUNKS : CHUNKS + 1, :] = jnp.broadcast_to(own_score, (1, LANES))
 
     own_lat = nn_dot(nope[1:], w_uk_ref[1, own_head]).astype(bf16)
-    latent = deep_ref[0, own_req, :LATENT]
-    rotary = deep_ref[0, own_req, LATENT:]
+    latent = deep_ref[:LATENT]
+    rotary = deep_ref[LATENT:]
     score = (nn_dot(own_lat, latent) + nn_dot(rope[1:], rotary)) * score_scale
-    live = deep_pos_ref[0, pl.ds(own_req, 1), :] < lengths_ref[own_req]
+    live = deep_pos_ref[0, pl.ds(own_req, 1), :] < length_of(lengths_ref, own_req)
     block_max = jnp.max(jnp.where(live, score, neg_fill), axis=1, keepdims=True)
     weight = jnp.where(live, jnp.exp(jnp.where(live, score - block_max, 0.0)), 0.0).astype(bf16)
     block_sum = jnp.sum(weight.astype(f32), axis=1, keepdims=True)
@@ -180,11 +200,16 @@
     far_factor = jnp.exp(block_max - top)
     total = own_factor + block_sum * far_factor
     mixed = ((own_factor * newlat[:, :LATENT] + block_out * far_factor) / total).astype(bf16)
-    aux_ref[CHUNKS + 1 : CHUNKS + 2, :] = nn_dot(mixed, w_uv_ref[1, own_head])
+    aux_ref[CHUNKS + 1 : CHUNKS + 2, :] = nn_dot(mixed, w_up_ref[1])
 
     for row, slot in ((CHUNKS + 2, holder), (CHUNKS + 3, holder + 1 - 2 * (holder % CORES))):
         req = slab_request(map_ref, slot).astype(f32)
         aux_ref[row : row + 1, :] = jnp.broadcast_to(req, (1, LANES))
+
+    shape = chips_ref.shape
+    place = iota(shape, 1) == own_req * SLABS_REQ + iota(shape, 0)
+    slots = jnp.sum(jnp.where(place, map_ref[...], 0), axis=1, keepdims=True)
+    chips_ref[...] = jnp.broadcast_to(slots // CORES, shape)
 
 
 def merge_kernel(keep_ref, far_ref, aux_ref, send_ref):
@@ -209,16 +234,14 @@
         send_ref[b * rows : (b + 1) * rows, :] = jnp.where(near_req == b, near, far).astype(bf16)
 
 
-def combine_kernel(idx_ref, map_ref, got_ref, aux_ref, w_uv_ref, out_ref):
-    holder = idx_ref[0]
-    own_req = holder // HEADS
-    own_head = holder % HEADS
+def combine_kernel(chips_ref, got_ref, aux_ref, w_up_ref, out_ref):
     own = aux_ref[...]
+    chips = chips_ref[...]
     own_score = own[CHUNKS : CHUNKS + 1]
     messages, levels = [], []
     top = own_score
     for s in range(SLABS_REQ):
-        chip = map_ref[0, own_req * SLABS_REQ + s] // CORES
+        chip = chips[s, 0]
         message = got_ref[pl.ds(pl.multiple_of(chip * MSG, MSG), MSG), :].astype(f32)
         level = message_level(message)
         messages.append(message)
@@ -232,21 +255,23 @@
         mixed = mixed + factor * message
     mixed = (mixed / total).astype(bf16).astype(f32)
     row = jnp.concatenate([mixed[j : j + 1] for j in range(CHUNKS)], axis=1).astype(bf16)
-    out = jnp.concatenate([nn_dot(row, w_uv_ref[0, own_head]), own[CHUNKS + 1 : CHUNKS + 2]], axis=0)
+    out = jnp.concatenate([nn_dot(row, w_up_ref[0]), own[CHUNKS + 1 : CHUNKS + 2]], axis=0)
     out_ref[0] = out.astype(bf16)
 
 
 VMEM = pl.BlockSpec(memory_space=pltpu.VMEM)
 SMEM = pl.BlockSpec(memory_space=pltpu.SMEM)
-
-
-def call(kernel, out_shape, in_specs, flops):
+ANY = pl.BlockSpec(memory_space=pl.ANY)
+
+
+def call(kernel, out_shape, in_specs, flops, scratch_shapes=()):
     many = isinstance(out_shape, tuple)
     return pl.pallas_call(
         kernel,
         out_shape=out_shape,
         in_specs=in_specs,
         out_specs=(VMEM,) * len(out_shape) if many else VMEM,
+        scratch_shapes=scratch_shapes,
         compiler_params=pltpu.CompilerParams(vmem_limit_bytes=12 << 20),
         cost_estimate=pl.CostEstimate(flops=flops, bytes_accessed=1 << 20, transcendentals=0),
     )
@@ -288,19 +313,42 @@
     )(holder, query, far_nope, far_rope)
     queries = exchanged(queries, CORES * 2)
     block = shape((HEADS // CORES * MSG, LANES), bf16)
-    keep, give = call(attend_kernel, (block, block), [SMEM, SMEM] + [VMEM] * 5, 1 << 24)(
-        holder, lengths, queries, w_uk, shallow_cache, slot_positions, slab_map
+    lengths = lengths.reshape(1, -1)
+    keep, give, deep, w_up = call(
+        attend_kernel,
+        (
+            block,
+            block,
+            shape(deep_cache.shape[2:], bf16),
+            shape((w_uv.shape[0], *w_uv.shape[2:]), bf16),
+        ),
+        [SMEM] + [VMEM] * 6 + [ANY] * 2,
+        1 << 24,
+        [pltpu.SemaphoreType.DMA((3,))],
+    )(
+        holder,
+        lengths,
+        queries,
+        w_uk,
+        shallow_cache,
+        slot_positions,
+        slab_map,
+        pltpu.with_memory_space_constraint(deep_cache, pltpu.HBM),
+        pltpu.with_memory_space_constraint(w_uv, pltpu.HBM),
     )
     far = swapped(give)
-    aux = call(own_kernel, shape((MSG, LANES), f32), [SMEM, SMEM] + [VMEM] * 7, 1 << 24)(
-        holder, lengths, query, w_uk, w_uv, new_latent, slab_map, deep_cache, deep_positions
-    )
+    aux, slab_chips = call(
+        own_kernel,
+        (shape((MSG, LANES), f32), shape((SLABS_REQ, LANES), jnp.int32)),
+        [SMEM] + [VMEM] * 8,
+        1 << 24,
+    )(holder, lengths, query, w_uk, w_up, new_latent, slab_map, deep, deep_positions)
     partials = call(merge_kernel, shape((chips * MSG, LANES), bf16), [VMEM] * 3, 1 << 20)(
         keep, far, aux
     )
     partials = exchanged(partials, MSG)
-    rows = call(combine_kernel, shape(q_nope.shape, bf16), [SMEM, SMEM] + [VMEM] * 3, 1 << 20)(
-        holder, slab_map, partials, aux, w_uv
+    rows = call(combine_kernel, shape(q_nope.shape, bf16), [VMEM] * 4, 1 << 20)(
+        slab_chips, partials, aux, w_up
     )
     return rows.swapaxes(0, 1)
 

time: 60.3 us -> 59 us (0.978)
  Pallas kernels: 4.49 us -> 3.63 us
    pallas_call x3, Pallas kernels: 4.36 us -> 3.51 us  [the longest x1 2.08 us: shards(): call(attend_kernel, (block, block, shape(deep_cache.shape[2:], bf16), sha...]
  transfers between devices with their start and end apart: 3 -> 3, of which waited for: 1 -> 2; matrix products, arithmetic and copies ran while one was open for 1% -> 1% of each run, Pallas kernels for 2% -> 1%
where the time goes in v4:
time: 59 us; the launch traced here: 58.8 us
  blocking collectives  31.7 us (54%)
  starting transfers between devices  21.9 us (37%)
  Pallas kernels  3.63 us (6%)
  waiting for transfers between devices  0.74 us (1%)
  other arithmetic  0.68 us (1%)
    all_to_all x2, blocking collectives, exchanged(): return lax.all_to_all(tiles, 'chips', 0, 0, tiled=True).reshape(rows.shape)  31.7 us
    ppermute x3, starting transfers between devices, swapped(): lax.ppermute(x, 'cores', [(k, (k + 1) % CORES) for k in range(CORES)])  21.9 us
    pallas_call x1, Pallas kernels, shards(): call(attend_kernel, (block, block, shape(deep_cache.shape[2:], bf16), sha...  2.08 us
  transfers between devices with their start and end apart: 3, of which 2 were waited for; matrix products, arithmetic and copies ran while one was open for 1% of the time, Pallas kernels for 1%

profile of v4, /device:TPU:513, one launch (start us, length us, event | category | flops | bytes accessed | tf_op | source)
XLA Modules:
  0.0 58.8 jit_solution(13738922625231910955)
XLA Ops:
  0.0 20.4 %collective-permute-start = (bf16[1,2,128]{2,1,0:T(2,128)(2,1)}, bf16[1,2,128]{2,1,0:T(2,128)(2,1)S(1)}, u32[]{:S(2)}, u32[]{:S(2)}) collective-permute-start(bf16[1,2,128]{2,1,0:T(2,128)(2,1)} %bitcast.21), channel_id=1, source_target_pairs={{0,1},{1,0},{2,3},{3,2},{4,5},{5,4},{6,7},{7,6},{8,9},{9,8},{10,11... | collective-permute-start | bytes 1544 | tf_op jit(solution)/shard_map/ppermute | solution.py:287
  20.4 0.0 collective-permute-start.1
  20.4 0.7 %pad_maximum_fusion.query_ref = bf16[1,2,192]{2,1,0:T(2,128)(2,1)S(1)} fusion(bf16[1,2,64]{2,1,0:T(2,128)(2,1)} %bitcast.20, bf16[1,2,128]{2,1,0:T(2,128)(2,1)} %bitcast.22), kind=kLoop, calls=%fused_computation | loop fusion | flops 1536 | bytes 1536 | tf_op jit(solution)/shard_map/concatenate | solution.py:310
  21.1 0.6 %collective-permute-done.1.far_rope_ref = bf16[1,2,64]{2,1,0:T(2,128)(2,1)S(1)} collective-permute-done((bf16[1,2,64]{2,1,0:T(2,128)(2,1)}, bf16[1,2,64]{2,1,0:T(2,128)(2,1)S(1)}, u32[]{:S(2)}, u32[]{:S(2)}) %collective-permute-start.1) | collective-permute-done | bytes 288 | tf_op jit(solution)/shard_map/ppermute | solution.py:287
  21.7 0.0 collective-permute-done.far_nope_ref
  21.7 0.0 copy-start
  21.7 0.0 copy-start.1
  21.7 0.0 copy-start.4
  21.7 0.0 copy-start.5
  21.7 0.0 copy-start.6
  21.8 15.8 %all_to_all.10 = bf16[64,4,128]{2,1,0:T(4,128)(2,1)S(1)} all-to-all(bf16[64,4,128]{2,1,0:T(4,128)(2,1)S(1)} %bitcast.15), channel_id=1, replica_groups=mesh['groups'=2,'chips'=64,'cores'=2] {'chips'}, dimensions={0} | all-to-all | bytes 131072 | tf_op jit(solution)/shard_map/all_to_all | solution.py:283
  37.6 0.0 copy-done
  37.6 0.0 copy-done.1
  37.6 0.0 copy-done.4
  37.6 0.0 copy-done.5
  37.7 0.0 copy-done.6
  37.7 0.0 copy-start.2
  37.7 0.0 copy-start.3
  37.7 2.1 %shard_map.110 = (bf16[64,128]{1,0:T(8,128)(2,1)S(1)}, bf16[64,128]{1,0:T(8,128)(2,1)S(1)}, bf16[576,256]{1,0:T(8,128)(2,1)S(1)}, bf16[2,512,128]{2,1,0:T(8,128)(2,1)S(1)}) custom-call(s32[1]{0:T(128)} %bitcast.idx_ref, s32[1,8]{1,0:T(1,128)S(1)} %bitcast.16, bf16[256,128]{1,0:T(8,128)(2,1)S(1)} %bitcast.14, bf16[2,16,128,512]{3,2,1,0:T(8,128)(2,1)S(1)} %copy-done, ...), custom_call_target="tpu_custom_call" | custom-call | flops 16777216 | bytes 1048576 | tf_op jit(solution)/shard_map/pallas_call | solution.py:317
  39.8 1.5 %collective-permute-start.2 = (bf16[64,128]{1,0:T(8,128)(2,1)S(1)}, bf16[64,128]{1,0:T(8,128)(2,1)S(1)}, u32[]{:S(2)}, u32[]{:S(2)}) collective-permute-start(bf16[64,128]{1,0:T(8,128)(2,1)S(1)} %get-tuple-element.15), channel_id=1, source_target_pairs={{0,1},{1,0},{2,3},{3,2},{4,5},{5,4},{6,7},{7,6},{8,9},{9,8},{10,11... | collective-permute-start | bytes 49160 | tf_op jit(solution)/shard_map/ppermute | solution.py:287
  41.3 0.0 copy-done.2
  41.3 0.0 copy-done.3
  41.3 0.7 %shard_map.111 = (f32[8,128]{1,0:T(8,128)S(1)}, s32[16,128]{1,0:T(8,128)S(1)}) custom-call(s32[1]{0:T(128)} %bitcast.idx_ref, s32[1,8]{1,0:T(1,128)S(1)} %bitcast.17, bf16[1,2,192]{2,1,0:T(2,128)(2,1)S(1)} %pad_maximum_fusion.query_ref, bf16[2,16,128,512]{3,2,1,0:T(8,128)(2,1)S(1)} %copy-done, bf16[2,512,128]{2,1,0:T(8,128)(2,1)S(1)} %get-tuple-element.11.w_up_ref, ...), custom_call_target="tpu_custom_call" | custom-call | flops 16777216 | bytes 1048576 | tf_op jit(solution)/shard_map/pallas_call | solution.py:340
  42.0 0.1 collective-permute-done.2.far_ref
  42.1 0.1 shard_map.112
  42.2 15.9 %all_to_all.11 = bf16[64,8,128]{2,1,0:T(8,128)(2,1)S(1)} all-to-all(bf16[64,8,128]{2,1,0:T(8,128)(2,1)S(1)} %bitcast.13), channel_id=1, replica_groups=mesh['groups'=2,'chips'=64,'cores'=2] {'chips'}, dimensions={0} | all-to-all | bytes 262144 | tf_op jit(solution)/shard_map/all_to_all | solution.py:283
  58.1 0.7 %shard_map.113 = bf16[1,2,128]{2,1,0:T(2,128)(2,1)} custom-call(s32[16,128]{1,0:T(8,128)S(1)} %get-tuple-element.13.chips_ref, bf16[512,128]{1,0:T(8,128)(2,1)S(1)} %bitcast.12, f32[8,128]{1,0:T(8,128)S(1)} %get-tuple-element.16.aux_ref, bf16[2,512,128]{2,1,0:T(8,128)(2,1)S(1)} %get-tuple-element.11.w_up_ref), custom_call_target="tpu_custom_call" | custom-call | flops 1048576 | bytes 1048576 | tf_op jit(solution)/shard_map/pallas_call | solution.py:350
  (1 shorter events, 0.0 us)
Async XLA Ops:
  0.0 21.7 %collective-permute-start = (bf16[1,2,128]{2,1,0:T(2,128)(2,1)}, bf16[1,2,128]{2,1,0:T(2,128)(2,1)S(1)}, u32[]{:S(2)}, u32[]{:S(2)}) collective-permute-start(bf16[1,2,128]{2,1,0:T(2,128)(2,1)} %bitcast.21), channel_id=1, source_target_pairs={{0,1},{1,0},{2,3},{3,2},{4,5},{5,4},{6,7},{7,6},{8,9},{9,8},{10,11... | collective-permute-start | bytes 1544 | tf_op jit(solution)/shard_map/ppermute | solution.py:287
  20.4 1.3 %collective-permute-start.1 = (bf16[1,2,64]{2,1,0:T(2,128)(2,1)}, bf16[1,2,64]{2,1,0:T(2,128)(2,1)S(1)}, u32[]{:S(2)}, u32[]{:S(2)}) collective-permute-start(bf16[1,2,64]{2,1,0:T(2,128)(2,1)} %bitcast.19), channel_id=1, source_target_pairs={{0,1},{1,0},{2,3},{3,2},{4,5},{5,4},{6,7},{7,6},{8,9},{9,8},{10,11... | collective-permute-start | bytes 776 | tf_op jit(solution)/shard_map/ppermute | solution.py:287
  21.7 15.9 %copy-start = (bf16[2,16,128,512]{3,2,1,0:T(8,128)(2,1)S(1)}, bf16[2,16,128,512]{3,2,1,0:T(8,128)(2,1)}, u32[]{:S(2)}) copy-start(bf16[2,16,128,512]{3,2,1,0:T(8,128)(2,1)} %w_uk_ref.3) | copy-start | bytes 12582916
  21.7 15.9 %copy-start.1 = (bf16[1,1,512,576]{2,3,1,0:T(8,128)(2,1)S(1)}, bf16[1,1,512,576]{2,3,1,0:T(8,128)(2,1)}, u32[]{:S(2)}) copy-start(bf16[1,1,512,576]{2,3,1,0:T(8,128)(2,1)} %param.16) | copy-start | bytes 1769476
  21.7 15.9 %copy-start.4 = (s32[1,1,512]{2,1,0:T(1,128)S(1)}, s32[1,1,512]{2,1,0:T(1,128)}, u32[]{:S(2)}) copy-start(s32[1,1,512]{2,1,0:T(1,128)} %slab_pos_ref.1) | copy-start | bytes 6148
  21.7 15.9 %copy-start.5 = (s32[8]{0:T(128)S(1)}, s32[8]{0:T(128)}, u32[]{:S(2)}) copy-start(s32[8]{0:T(128)} %param.21) | copy-start | bytes 100
  21.7 15.9 %copy-start.6 = (s32[1,128]{1,0:T(1,128)S(1)}, s32[1,128]{1,0:T(1,128)}, u32[]{:S(2)}) copy-start(s32[1,128]{1,0:T(1,128)} %map_ref.3) | copy-start | bytes 1540
  37.7 3.6 %copy-start.2 = (bf16[2,8,576]{2,1,0:T(8,128)(2,1)S(1)}, bf16[2,8,576]{2,1,0:T(8,128)(2,1)}, u32[]{:S(2)}) copy-start(bf16[2,8,576]{2,1,0:T(8,128)(2,1)} %newlat_ref.1) | copy-start | bytes 55300
  37.7 3.6 %copy-start.3 = (s32[1,8,256]{2,1,0:T(8,128)S(1)}, s32[1,8,256]{2,1,0:T(8,128)}, u32[]{:S(2)}) copy-start(s32[1,8,256]{2,1,0:T(8,128)} %deep_pos_ref.1) | copy-start | bytes 24580
  39.8 2.3 %collective-permute-start.2 = (bf16[64,128]{1,0:T(8,128)(2,1)S(1)}, bf16[64,128]{1,0:T(8,128)(2,1)S(1)}, u32[]{:S(2)}, u32[]{:S(2)}) collective-permute-start(bf16[64,128]{1,0:T(8,128)(2,1)S(1)} %get-tuple-element.15), channel_id=1, source_target_pairs={{0,1},{1,0},{2,3},{3,2},{4,5},{5,4},{6,7},{7,6},{8,9},{9,8},{10,11... | collective-permute-start | bytes 49160 | tf_op jit(solution)/shard_map/ppermute | solution.py:287

commit v5 on v3

--- a/solution.py
+++ b/solution.py
@@ -76,6 +76,12 @@
     owners = map_ref[...]
     place = iota(owners.shape, 1) // SLABS_REQ
     return jnp.sum(jnp.where(owners == slot, place, 0), axis=1, keepdims=True)
+
+
+def length_of(lengths_ref, req):
+    lengths = lengths_ref[...]
+    mine = jnp.where(iota(lengths.shape, 1) == req, lengths, 0)
+    return jnp.sum(mine, axis=1, keepdims=True)
 
 
 def attend_kernel(
@@ -92,7 +98,6 @@
     holder = idx_ref[0]
     core = holder % CORES
     req_v = slab_request(map_ref, holder)
-    req = jnp.sum(req_v)
 
     shape = (2 * HEADS, got_ref.shape[0])
     part = iota(shape, 0)
@@ -111,7 +116,7 @@
     latent = slab_ref[0, 0, :LATENT]
     rotary = slab_ref[0, 0, LATENT:]
     score = (nn_dot(q_lat, latent) + nn_dot(q_rope, rotary)) * score_scale
-    live = slab_pos_ref[0] < lengths_ref[req]
+    live = slab_pos_ref[0] < length_of(lengths_ref, req_v)
     top = jnp.max(jnp.where(live, score, neg_fill), axis=1, keepdims=True)
     weight = jnp.where(live, jnp.exp(jnp.where(live, score - top, 0.0)), 0.0).astype(bf16)
     total = jnp.sum(weight.astype(f32), axis=1, keepdims=True)
@@ -145,6 +150,7 @@
     deep_ref,
     deep_pos_ref,
     aux_ref,
+    chips_ref,
 ):
     holder = idx_ref[0]
     own_req = holder // HEADS
@@ -165,7 +171,7 @@
     latent = deep_ref[0, own_req, :LATENT]
     rotary = deep_ref[0, own_req, LATENT:]
     score = (nn_dot(own_lat, latent) + nn_dot(rope[1:], rotary)) * score_scale
-    live = deep_pos_ref[0, pl.ds(own_req, 1), :] < lengths_ref[own_req]
+    live = deep_pos_ref[0, pl.ds(own_req, 1), :] < length_of(lengths_ref, own_req)
     block_max = jnp.max(jnp.where(live, score, neg_fill), axis=1, keepdims=True)
     weight = jnp.where(live, jnp.exp(jnp.where(live, score - block_max, 0.0)), 0.0).astype(bf16)
     block_sum = jnp.sum(weight.astype(f32), axis=1, keepdims=True)
@@ -185,6 +191,11 @@
     for row, slot in ((CHUNKS + 2, holder), (CHUNKS + 3, holder + 1 - 2 * (holder % CORES))):
         req = slab_request(map_ref, slot).astype(f32)
         aux_ref[row : row + 1, :] = jnp.broadcast_to(req, (1, LANES))
+
+    shape = chips_ref.shape
+    place = iota(shape, 1) == own_req * SLABS_REQ + iota(shape, 0)
+    slots = jnp.sum(jnp.where(place, map_ref[...], 0), axis=1, keepdims=True)
+    chips_ref[...] = jnp.broadcast_to(slots // CORES, shape)
 
 
 def merge_kernel(keep_ref, far_ref, aux_ref, send_ref):
@@ -209,16 +220,15 @@
         send_ref[b * rows : (b + 1) * rows, :] = jnp.where(near_req == b, near, far).astype(bf16)
 
 
-def combine_kernel(idx_ref, map_ref, got_ref, aux_ref, w_uv_ref, out_ref):
-    holder = idx_ref[0]
-    own_req = holder // HEADS
-    own_head = holder % HEADS
+def combine_kernel(idx_ref, chips_ref, got_ref, aux_ref, w_uv_ref, out_ref):
+    own_head = idx_ref[0] % HEADS
     own = aux_ref[...]
+    chips = chips_ref[...]
     own_score = own[CHUNKS : CHUNKS + 1]
     messages, levels = [], []
     top = own_score
     for s in range(SLABS_REQ):
-        chip = map_ref[0, own_req * SLABS_REQ + s] // CORES
+        chip = chips[s, 0]
         message = got_ref[pl.ds(pl.multiple_of(chip * MSG, MSG), MSG), :].astype(f32)
         level = message_level(message)
         messages.append(message)
@@ -288,19 +298,25 @@
     )(holder, query, far_nope, far_rope)
     queries = exchanged(queries, CORES * 2)
     block = shape((HEADS // CORES * MSG, LANES), bf16)
-    keep, give = call(attend_kernel, (block, block), [SMEM, SMEM] + [VMEM] * 5, 1 << 24)(
+    lengths = lengths.reshape(1, -1)
+    keep, give = call(attend_kernel, (block, block), [SMEM] + [VMEM] * 6, 1 << 24)(
         holder, lengths, queries, w_uk, shallow_cache, slot_positions, slab_map
     )
     far = swapped(give)
-    aux = call(own_kernel, shape((MSG, LANES), f32), [SMEM, SMEM] + [VMEM] * 7, 1 << 24)(
+    aux, slab_chips = call(
+        own_kernel,
+        (shape((MSG, LANES), f32), shape((SLABS_REQ, LANES), jnp.int32)),
+        [SMEM] + [VMEM] * 8,
+        1 << 24,
+    )(
         holder, lengths, query, w_uk, w_uv, new_latent, slab_map, deep_cache, deep_positions
     )
     partials = call(merge_kernel, shape((chips * MSG, LANES), bf16), [VMEM] * 3, 1 << 20)(
         keep, far, aux
     )
     partials = exchanged(partials, MSG)
-    rows = call(combine_kernel, shape(q_nope.shape, bf16), [SMEM, SMEM] + [VMEM] * 3, 1 << 20)(
-        holder, slab_map, partials, aux, w_uv
+    rows = call(combine_kernel, shape(q_nope.shape, bf16), [SMEM] + [VMEM] * 4, 1 << 20)(
+        holder, slab_chips, partials, aux, w_uv
     )
     return rows.swapaxes(0, 1)
 

time: 60.3 us -> 58.4 us (0.968)
  Pallas kernels: 4.49 us -> 2.82 us
    pallas_call x3, Pallas kernels: 4.36 us -> 2.7 us  [the longest x1 1.27 us: shards(): call(attend_kernel, (block, block), [SMEM] + [VMEM] * 6, 1 << 24)]
  transfers between devices with their start and end apart: 3 -> 3, of which waited for: 1 -> 2; matrix products, arithmetic and copies ran while one was open for 1% -> 1% of each run, Pallas kernels for 2% -> 1%
where the time goes in v5:
time: 58.4 us; the launch traced here: 58.3 us
  blocking collectives  32 us (55%)
  starting transfers between devices  21.9 us (38%)
  Pallas kernels  2.82 us (5%)
  waiting for transfers between devices  0.73 us (1%)
  other arithmetic  0.68 us (1%)
    all_to_all x2, blocking collectives, exchanged(): return lax.all_to_all(tiles, 'chips', 0, 0, tiled=True).reshape(rows.shape)  32 us
    ppermute x3, starting transfers between devices, swapped(): lax.ppermute(x, 'cores', [(k, (k + 1) % CORES) for k in range(CORES)])  21.9 us
    pallas_call x1, Pallas kernels, shards(): call(attend_kernel, (block, block), [SMEM] + [VMEM] * 6, 1 << 24)  1.27 us
  transfers between devices with their start and end apart: 3, of which 2 were waited for; matrix products, arithmetic and copies ran while one was open for 1% of the time, Pallas kernels for 1%

profile of v5, /device:TPU:513, one launch (start us, length us, event | category | flops | bytes accessed | tf_op | source)
XLA Modules:
  0.0 58.3 jit_solution(9117050546484088856)
XLA Ops:
  0.0 20.4 %collective-permute-start = (bf16[1,2,128]{2,1,0:T(2,128)(2,1)}, bf16[1,2,128]{2,1,0:T(2,128)(2,1)S(1)}, u32[]{:S(2)}, u32[]{:S(2)}) collective-permute-start(bf16[1,2,128]{2,1,0:T(2,128)(2,1)} %bitcast.21), channel_id=1, source_target_pairs={{0,1},{1,0},{2,3},{3,2},{4,5},{5,4},{6,7},{7,6},{8,9},{9,8},{10,11... | collective-permute-start | bytes 1544 | tf_op jit(solution)/shard_map/ppermute | solution.py:272
  20.4 0.0 collective-permute-start.1
  20.4 0.7 %pad_maximum_fusion.query_ref = bf16[1,2,192]{2,1,0:T(2,128)(2,1)S(1)} fusion(bf16[1,2,64]{2,1,0:T(2,128)(2,1)} %bitcast.20, bf16[1,2,128]{2,1,0:T(2,128)(2,1)} %bitcast.22), kind=kLoop, calls=%fused_computation | loop fusion | flops 1536 | bytes 1536 | tf_op jit(solution)/shard_map/concatenate | solution.py:295
  21.1 0.6 %collective-permute-done.1.far_rope_ref = bf16[1,2,64]{2,1,0:T(2,128)(2,1)S(1)} collective-permute-done((bf16[1,2,64]{2,1,0:T(2,128)(2,1)}, bf16[1,2,64]{2,1,0:T(2,128)(2,1)S(1)}, u32[]{:S(2)}, u32[]{:S(2)}) %collective-permute-start.1) | collective-permute-done | bytes 288 | tf_op jit(solution)/shard_map/ppermute | solution.py:272
  21.7 0.0 collective-permute-done.far_nope_ref
  21.7 0.0 copy-start
  21.7 0.0 copy-start.3
  21.7 0.0 copy-start.6
  21.7 0.0 copy-start.7
  21.7 0.0 copy-start.8
  21.7 0.0 copy-start.2
  21.8 0.0 copy-start.1
  21.8 0.0 copy-start.4
  21.8 0.0 copy-start.5
  21.9 16.1 %all_to_all.10 = bf16[64,4,128]{2,1,0:T(4,128)(2,1)S(1)} all-to-all(bf16[64,4,128]{2,1,0:T(4,128)(2,1)S(1)} %bitcast.16), channel_id=1, replica_groups=mesh['groups'=2,'chips'=64,'cores'=2] {'chips'}, dimensions={0} | all-to-all | bytes 131072 | tf_op jit(solution)/shard_map/all_to_all | solution.py:268
  38.0 0.0 copy-done
  38.0 0.0 copy-done.3
  38.0 0.0 copy-done.6
  38.0 0.0 copy-done.7
  38.0 0.0 copy-done.8
  38.0 1.3 %shard_map.111 = (bf16[64,128]{1,0:T(8,128)(2,1)S(1)}, bf16[64,128]{1,0:T(8,128)(2,1)S(1)}) custom-call(s32[1]{0:T(128)} %bitcast.idx_ref, s32[1,8]{1,0:T(1,128)S(1)} %bitcast.17, bf16[256,128]{1,0:T(8,128)(2,1)S(1)} %bitcast.15, bf16[2,16,128,512]{3,2,1,0:T(8,128)(2,1)S(1)} %copy-done, bf16[1,1,576,512]{3,2,1,0:T(8,128)(2,1)S(1)} %bitcast.12, ...), custom_call_target="tpu_custom_call" | custom-call | flops 16777216 | bytes 1048576 | tf_op jit(solution)/shard_map/pallas_call | solution.py:302
  39.3 1.5 %collective-permute-start.2 = (bf16[64,128]{1,0:T(8,128)(2,1)S(1)}, bf16[64,128]{1,0:T(8,128)(2,1)S(1)}, u32[]{:S(2)}, u32[]{:S(2)}) collective-permute-start(bf16[64,128]{1,0:T(8,128)(2,1)S(1)} %get-tuple-element.11), channel_id=1, source_target_pairs={{0,1},{1,0},{2,3},{3,2},{4,5},{5,4},{6,7},{7,6},{8,9},{9,8},{10,11... | collective-permute-start | bytes 49160 | tf_op jit(solution)/shard_map/ppermute | solution.py:272
  40.8 0.0 copy-done.2
  40.8 0.0 copy-done.1
  40.8 0.0 copy-done.4
  40.8 0.0 copy-done.5
  40.8 0.7 %shard_map.109 = (f32[8,128]{1,0:T(8,128)S(1)}, s32[16,128]{1,0:T(8,128)S(1)}) custom-call(s32[1]{0:T(128)} %bitcast.idx_ref, s32[1,8]{1,0:T(1,128)S(1)} %bitcast.18, bf16[1,2,192]{2,1,0:T(2,128)(2,1)S(1)} %pad_maximum_fusion.query_ref, bf16[2,16,128,512]{3,2,1,0:T(8,128)(2,1)S(1)} %copy-done, bf16[2,16,512,128]{3,2,1,0:T(8,128)(2,1)S(1)} %copy-done.1, ...), custom_call_target="tpu_custom_call" | custom-call | flops 16777216 | bytes 1048576 | tf_op jit(solution)/shard_map/pallas_call | solution.py:306
  41.5 0.1 collective-permute-done.2.far_ref
  41.6 0.1 shard_map.112
  41.7 15.9 %all_to_all.11 = bf16[64,8,128]{2,1,0:T(8,128)(2,1)S(1)} all-to-all(bf16[64,8,128]{2,1,0:T(8,128)(2,1)S(1)} %bitcast.14), channel_id=1, replica_groups=mesh['groups'=2,'chips'=64,'cores'=2] {'chips'}, dimensions={0} | all-to-all | bytes 262144 | tf_op jit(solution)/shard_map/all_to_all | solution.py:268
  57.5 0.7 %shard_map.113 = bf16[1,2,128]{2,1,0:T(2,128)(2,1)} custom-call(s32[1]{0:T(128)} %bitcast.idx_ref, s32[16,128]{1,0:T(8,128)S(1)} %get-tuple-element.9.chips_ref, bf16[512,128]{1,0:T(8,128)(2,1)S(1)} %bitcast.13, f32[8,128]{1,0:T(8,128)S(1)} %get-tuple-element.12.aux_ref, bf16[2,16,512,128]{3,2,1,0:T(8,128)(2,1)S(1)} %copy-done.1), custom_call_target="tpu_custom_call" | custom-call | flops 1048576 | bytes 1048576 | tf_op jit(solution)/shard_map/pallas_call | solution.py:318
  (1 shorter events, 0.0 us)
Async XLA Ops:
  0.0 21.7 %collective-permute-start = (bf16[1,2,128]{2,1,0:T(2,128)(2,1)}, bf16[1,2,128]{2,1,0:T(2,128)(2,1)S(1)}, u32[]{:S(2)}, u32[]{:S(2)}) collective-permute-start(bf16[1,2,128]{2,1,0:T(2,128)(2,1)} %bitcast.21), channel_id=1, source_target_pairs={{0,1},{1,0},{2,3},{3,2},{4,5},{5,4},{6,7},{7,6},{8,9},{9,8},{10,11... | collective-permute-start | bytes 1544 | tf_op jit(solution)/shard_map/ppermute | solution.py:272
  20.4 1.3 %collective-permute-start.1 = (bf16[1,2,64]{2,1,0:T(2,128)(2,1)}, bf16[1,2,64]{2,1,0:T(2,128)(2,1)S(1)}, u32[]{:S(2)}, u32[]{:S(2)}) collective-permute-start(bf16[1,2,64]{2,1,0:T(2,128)(2,1)} %bitcast.19), channel_id=1, source_target_pairs={{0,1},{1,0},{2,3},{3,2},{4,5},{5,4},{6,7},{7,6},{8,9},{9,8},{10,11... | collective-permute-start | bytes 776 | tf_op jit(solution)/shard_map/ppermute | solution.py:272
  21.7 16.2 %copy-start = (bf16[2,16,128,512]{3,2,1,0:T(8,128)(2,1)S(1)}, bf16[2,16,128,512]{3,2,1,0:T(8,128)(2,1)}, u32[]{:S(2)}) copy-start(bf16[2,16,128,512]{3,2,1,0:T(8,128)(2,1)} %w_uk_ref.3) | copy-start | bytes 12582916
  21.7 16.2 %copy-start.3 = (bf16[1,1,512,576]{2,3,1,0:T(8,128)(2,1)S(1)}, bf16[1,1,512,576]{2,3,1,0:T(8,128)(2,1)}, u32[]{:S(2)}) copy-start(bf16[1,1,512,576]{2,3,1,0:T(8,128)(2,1)} %param.16) | copy-start | bytes 1769476
  21.7 16.2 %copy-start.6 = (s32[1,1,512]{2,1,0:T(1,128)S(1)}, s32[1,1,512]{2,1,0:T(1,128)}, u32[]{:S(2)}) copy-start(s32[1,1,512]{2,1,0:T(1,128)} %slab_pos_ref.1) | copy-start | bytes 6148
  21.7 16.2 %copy-start.7 = (s32[8]{0:T(128)S(1)}, s32[8]{0:T(128)}, u32[]{:S(2)}) copy-start(s32[8]{0:T(128)} %param.21) | copy-start | bytes 100
  21.7 16.2 %copy-start.8 = (s32[1,128]{1,0:T(1,128)S(1)}, s32[1,128]{1,0:T(1,128)}, u32[]{:S(2)}) copy-start(s32[1,128]{1,0:T(1,128)} %map_ref.3) | copy-start | bytes 1540
  21.7 19.0 %copy-start.2 = (bf16[1,8,256,576]{2,3,1,0:T(8,128)(2,1)S(1)}, bf16[1,8,256,576]{2,3,1,0:T(8,128)(2,1)}, u32[]{:S(2)}) copy-start(bf16[1,8,256,576]{2,3,1,0:T(8,128)(2,1)} %param.19) | copy-start | bytes 7077892
  21.8 18.9 %copy-start.1 = (bf16[2,16,512,128]{3,2,1,0:T(8,128)(2,1)S(1)}, bf16[2,16,512,128]{3,2,1,0:T(8,128)(2,1)}, u32[]{:S(2)}) copy-start(bf16[2,16,512,128]{3,2,1,0:T(8,128)(2,1)} %w_uv_ref.3) | copy-start | bytes 12582916
  21.8 18.9 %copy-start.4 = (bf16[2,8,576]{2,1,0:T(8,128)(2,1)S(1)}, bf16[2,8,576]{2,1,0:T(8,128)(2,1)}, u32[]{:S(2)}) copy-start(bf16[2,8,576]{2,1,0:T(8,128)(2,1)} %newlat_ref.1) | copy-start | bytes 55300
  21.8 18.9 %copy-start.5 = (s32[1,8,256]{2,1,0:T(8,128)S(1)}, s32[1,8,256]{2,1,0:T(8,128)}, u32[]{:S(2)}) copy-start(s32[1,8,256]{2,1,0:T(8,128)} %deep_pos_ref.1) | copy-start | bytes 24580
  39.3 2.3 %collective-permute-start.2 = (bf16[64,128]{1,0:T(8,128)(2,1)S(1)}, bf16[64,128]{1,0:T(8,128)(2,1)S(1)}, u32[]{:S(2)}, u32[]{:S(2)}) collective-permute-start(bf16[64,128]{1,0:T(8,128)(2,1)S(1)} %get-tuple-element.11), channel_id=1, source_target_pairs={{0,1},{1,0},{2,3},{3,2},{4,5},{5,4},{6,7},{7,6},{8,9},{9,8},{10,11... | collective-permute-start | bytes 49160 | tf_op jit(solution)/shard_map/ppermute | solution.py:272

commit v6 on v5

--- a/solution.py
+++ b/solution.py
@@ -13,8 +13,7 @@
 NOPE = 128
 SLABS_REQ = 16
 LANES = 128
-CHUNKS = LATENT // LANES
-MSG = 8
+MSG = 2
 CORES = 2
 LOG_2 = math.log(2.0)
 
@@ -39,19 +38,6 @@
 def picked_row(rows, at):
     rows = rows.astype(f32)
     return jnp.sum(jnp.where(iota(rows.shape, 0) == at, rows, 0.0), axis=0, keepdims=True)
-
-
-def pieces(x):
-    out = []
-    for _ in range(3):
-        out.append(x.astype(bf16))
-        x = x - out[-1].astype(f32)
-    return out
-
-
-def message_level(message):
-    rows = [message[..., CHUNKS + j : CHUNKS + j + 1, :] for j in range(3)]
-    return rows[0] + (rows[1] + rows[2])
 
 
 def prep_kernel(idx_ref, query_ref, far_nope_ref, far_rope_ref, out_ref):
@@ -72,6 +58,12 @@
     out_ref[...] = rows.astype(bf16)
 
 
+def by_head(rows):
+    wide = jnp.concatenate([rows] * HEADS, axis=1)
+    diagonal = iota(wide.shape, 1) // rows.shape[1] == iota(wide.shape, 0)
+    return jnp.where(diagonal, wide, jnp.zeros_like(wide))
+
+
 def slab_request(map_ref, slot):
     owners = map_ref[...]
     place = iota(owners.shape, 1) // SLABS_REQ
@@ -89,11 +81,14 @@
     lengths_ref,
     got_ref,
     w_uk_ref,
+    w_uv_ref,
     slab_ref,
     slab_pos_ref,
     map_ref,
     keep_ref,
     give_ref,
+    up_ref,
+    level_ref,
 ):
     holder = idx_ref[0]
     core = holder % CORES
@@ -107,11 +102,7 @@
     rope_dim = slab_ref.shape[2] - LATENT
     q_nope, q_rope = q_all[:HEADS], q_all[HEADS:, :rope_dim]
 
-    wide = jnp.concatenate([q_nope] * HEADS, axis=1)
-    diagonal = iota(wide.shape, 1) // NOPE == iota(wide.shape, 0)
-    wide = jnp.where(diagonal, wide, jnp.zeros_like(wide))
-    w_uk = w_uk_ref[0].reshape(wide.shape[1], LATENT)
-    q_lat = nn_dot(wide, w_uk).astype(bf16)
+    q_lat = nn_dot(by_head(q_nope), w_uk_ref[0].reshape(-1, LATENT)).astype(bf16)
 
     latent = slab_ref[0, 0, :LATENT]
     rotary = slab_ref[0, 0, LATENT:]
@@ -124,19 +115,12 @@
     out = nt_dot(weight, latent) / safe
     level = jnp.where(total > 0.0, top + jnp.log(safe), neg_fill)
 
-    blocks = [out[:, j * LANES : (j + 1) * LANES].astype(bf16) for j in range(CHUNKS)]
-    blocks += pieces(jnp.broadcast_to(level, (HEADS, LANES)))
-    stacked = jnp.concatenate(blocks, axis=0)
-    shape = (HEADS * MSG, stacked.shape[0])
-    line, column = iota(shape, 0), iota(shape, 1)
-    half = HEADS // CORES * MSG
-    parity = jnp.where(line < half, core, 1 - core)
-    head = line % half // MSG * CORES + parity
-    wanted = (column == line % MSG * HEADS + head) & (line % MSG < len(blocks))
-    spread = jnp.where(wanted, 1.0, 0.0).astype(bf16)
-    message = nn_dot(spread, stacked).astype(bf16)
-    keep_ref[...] = message[:half]
-    give_ref[...] = message[half:]
+    up_ref[...] = nn_dot(by_head(out.astype(bf16)), w_uv_ref[0].reshape(-1, LANES))
+    level_ref[...] = jnp.broadcast_to(level, level_ref.shape)
+    half = HEADS // CORES
+    for ref, first in ((keep_ref, core), (give_ref, 1 - core)):
+        ref[:half] = up_ref[pl.ds(first, half, stride=CORES), :]
+        ref[half:] = level_ref[pl.ds(first, half, stride=CORES), :]
 
 
 def own_kernel(
@@ -163,9 +147,8 @@
         jnp.sum(own_lat * newlat[:, :LATENT], axis=1, keepdims=True)
         + jnp.sum(rope[:1].astype(f32) * newlat[:, LATENT:], axis=1, keepdims=True)
     ) * score_scale
-    for j in range(CHUNKS):
-        aux_ref[j : j + 1, :] = newlat[:, j * LANES : (j + 1) * LANES]
-    aux_ref[CHUNKS : CHUNKS + 1, :] = jnp.broadcast_to(own_score, (1, LANES))
+    aux_ref[0:1, :] = nn_dot(newlat[:, :LATENT].astype(bf16), w_uv_ref[0, own_head])
+    aux_ref[1:2, :] = jnp.broadcast_to(own_score, (1, LANES))
 
     own_lat = nn_dot(nope[1:], w_uk_ref[1, own_head]).astype(bf16)
     latent = deep_ref[0, own_req, :LATENT]
@@ -186,9 +169,9 @@
     far_factor = jnp.exp(block_max - top)
     total = own_factor + block_sum * far_factor
     mixed = ((own_factor * newlat[:, :LATENT] + block_out * far_factor) / total).astype(bf16)
-    aux_ref[CHUNKS + 1 : CHUNKS + 2, :] = nn_dot(mixed, w_uv_ref[1, own_head])
-
-    for row, slot in ((CHUNKS + 2, holder), (CHUNKS + 3, holder + 1 - 2 * (holder % CORES))):
+    aux_ref[2:3, :] = nn_dot(mixed, w_uv_ref[1, own_head])
+
+    for row, slot in ((3, holder), (4, holder + 1 - 2 * (holder % CORES))):
         req = slab_request(map_ref, slot).astype(f32)
         aux_ref[row : row + 1, :] = jnp.broadcast_to(req, (1, LANES))
 
@@ -199,64 +182,52 @@
 
 
 def merge_kernel(keep_ref, far_ref, aux_ref, send_ref):
-    near_req, far_req = aux_ref[CHUNKS + 2 : CHUNKS + 3, :], aux_ref[CHUNKS + 3 : CHUNKS + 4, :]
-    blocks = keep_ref.shape[0] // MSG
-    near = keep_ref[...].astype(f32).reshape(blocks, MSG, LANES)
-    far = far_ref[...].astype(f32).reshape(blocks, MSG, LANES)
-    near_level, far_level = message_level(near), message_level(far)
+    near_req, far_req = aux_ref[3:4, :], aux_ref[4:5, :]
+    half = keep_ref.shape[0] // 2
+    near, near_level = keep_ref[:half], keep_ref[half:]
+    far, far_level = far_ref[:half], far_ref[half:]
     top = jnp.maximum(near_level, far_level)
     near_factor, far_factor = jnp.exp(near_level - top), jnp.exp(far_level - top)
     total = near_factor + far_factor
     merged = (near_factor * near + far_factor * far) / total
     level = top + (jnp.log(total) - LOG_2)
-    line = iota(merged.shape, 1)
-    for j, piece in enumerate(pieces(level)):
-        merged = jnp.where(line == CHUNKS + j, piece.astype(f32), merged)
     same = near_req == far_req
-    near = jnp.where(same, merged, near).reshape(keep_ref.shape)
-    far = jnp.where(same, merged, far).reshape(keep_ref.shape)
-    rows = keep_ref.shape[0]
-    for b in range(send_ref.shape[0] // rows):
-        send_ref[b * rows : (b + 1) * rows, :] = jnp.where(near_req == b, near, far).astype(bf16)
-
-
-def combine_kernel(idx_ref, chips_ref, got_ref, aux_ref, w_uv_ref, out_ref):
-    own_head = idx_ref[0] % HEADS
-    own = aux_ref[...]
+    near, near_level = jnp.where(same, merged, near), jnp.where(same, level, near_level)
+    far, far_level = jnp.where(same, merged, far), jnp.where(same, level, far_level)
+    for b in range(send_ref.shape[0] // (half * MSG)):
+        mine = near_req == b
+        first = b * half * MSG
+        send_ref[pl.ds(first, half, stride=MSG), :] = jnp.where(mine, near, far)
+        send_ref[pl.ds(first + 1, half, stride=MSG), :] = jnp.where(mine, near_level, far_level)
+
+
+def combine_kernel(chips_ref, got_ref, aux_ref, out_ref):
     chips = chips_ref[...]
-    own_score = own[CHUNKS : CHUNKS + 1]
-    messages, levels = [], []
-    top = own_score
+    own_score = aux_ref[1:2, :]
+    values, levels = [aux_ref[0:1, :]], [own_score]
     for s in range(SLABS_REQ):
-        chip = chips[s, 0]
-        message = got_ref[pl.ds(pl.multiple_of(chip * MSG, MSG), MSG), :].astype(f32)
-        level = message_level(message)
-        messages.append(message)
-        levels.append(level)
-        top = jnp.maximum(top, level)
-    total = jnp.exp(own_score - top)
-    mixed = total * own
-    for message, level in zip(messages, levels):
-        factor = jnp.exp(level - top)
-        total = total + factor
-        mixed = mixed + factor * message
-    mixed = (mixed / total).astype(bf16).astype(f32)
-    row = jnp.concatenate([mixed[j : j + 1] for j in range(CHUNKS)], axis=1).astype(bf16)
-    out = jnp.concatenate([nn_dot(row, w_uv_ref[0, own_head]), own[CHUNKS + 1 : CHUNKS + 2]], axis=0)
-    out_ref[0] = out.astype(bf16)
+        row = chips[s, 0] * MSG
+        values.append(got_ref[pl.ds(row, 1), :])
+        levels.append(got_ref[pl.ds(row + 1, 1), :])
+    values, levels = jnp.concatenate(values, axis=0), jnp.concatenate(levels, axis=0)
+    factors = jnp.exp(levels - jnp.max(levels, axis=0, keepdims=True))
+    total = jnp.sum(factors, axis=0, keepdims=True)
+    attended = jnp.sum(factors * values, axis=0, keepdims=True) / total
+    out_ref[0] = jnp.concatenate([attended, aux_ref[2:3, :]], axis=0).astype(bf16)
 
 
 VMEM = pl.BlockSpec(memory_space=pltpu.VMEM)
 SMEM = pl.BlockSpec(memory_space=pltpu.SMEM)
 
 
-def call(kernel, out_shape, in_specs, flops):
+def call(kernel, out_shape, in_specs, flops, scratch_shapes=()):
     many = isinstance(out_shape, tuple)
     return pl.pallas_call(
         kernel,
         out_shape=out_shape,
         in_specs=in_specs,
         out_specs=(VMEM,) * len(out_shape) if many else VMEM,
+        scratch_shapes=scratch_shapes,
         compiler_params=pltpu.CompilerParams(vmem_limit_bytes=12 << 20),
         cost_estimate=pl.CostEstimate(flops=flops, bytes_accessed=1 << 20, transcendentals=0),
     )
@@ -297,26 +268,30 @@
         prep_kernel, shape((chips * CORES * 2, LANES), bf16), [SMEM] + [VMEM] * 3, 1 << 33
     )(holder, query, far_nope, far_rope)
     queries = exchanged(queries, CORES * 2)
-    block = shape((HEADS // CORES * MSG, LANES), bf16)
+    block = shape((HEADS // CORES * MSG, LANES), f32)
     lengths = lengths.reshape(1, -1)
-    keep, give = call(attend_kernel, (block, block), [SMEM] + [VMEM] * 6, 1 << 24)(
-        holder, lengths, queries, w_uk, shallow_cache, slot_positions, slab_map
-    )
+    keep, give = call(
+        attend_kernel,
+        (block, block),
+        [SMEM] + [VMEM] * 7,
+        1 << 24,
+        [pltpu.VMEM((HEADS, LANES), f32)] * 2,
+    )(holder, lengths, queries, w_uk, w_uv, shallow_cache, slot_positions, slab_map)
     far = swapped(give)
     aux, slab_chips = call(
         own_kernel,
-        (shape((MSG, LANES), f32), shape((SLABS_REQ, LANES), jnp.int32)),
+        (shape((8, LANES), f32), shape((SLABS_REQ, LANES), jnp.int32)),
         [SMEM] + [VMEM] * 8,
         1 << 24,
     )(
         holder, lengths, query, w_uk, w_uv, new_latent, slab_map, deep_cache, deep_positions
     )
-    partials = call(merge_kernel, shape((chips * MSG, LANES), bf16), [VMEM] * 3, 1 << 20)(
+    partials = call(merge_kernel, shape((chips * MSG, LANES), f32), [VMEM] * 3, 1 << 20)(
         keep, far, aux
     )
     partials = exchanged(partials, MSG)
-    rows = call(combine_kernel, shape(q_nope.shape, bf16), [SMEM] + [VMEM] * 4, 1 << 20)(
-        holder, slab_chips, partials, aux, w_uv
+    rows = call(combine_kernel, shape(q_nope.shape, bf16), [VMEM] * 3, 1 << 20)(
+        slab_chips, partials, aux
     )
     return rows.swapaxes(0, 1)
 

time: 58.4 us -> 58.2 us (level)
  no operation moved by 1% of the time
where the time goes in v6:
time: 58.2 us; the launch traced here: 58.1 us
  blocking collectives  31.6 us (54%)
  starting transfers between devices  21.9 us (38%)
  Pallas kernels  2.99 us (5%)
  waiting for transfers between devices  0.71 us (1%)
  other arithmetic  0.68 us (1%)
    all_to_all x2, blocking collectives, exchanged(): return lax.all_to_all(tiles, 'chips', 0, 0, tiled=True).reshape(rows.shape)  31.6 us
    ppermute x3, starting transfers between devices, swapped(): lax.ppermute(x, 'cores', [(k, (k + 1) % CORES) for k in range(CORES)])  21.9 us
    pallas_call x1, Pallas kernels, shards(): call(attend_kernel, (block, block), [SMEM] + [VMEM] * 7, 1 << 24, [pltpu....  1.61 us
  transfers between devices with their start and end apart: 3, of which 2 were waited for; matrix products, arithmetic and copies ran while one was open for 1% of the time, Pallas kernels for 1%

profile of v6, /device:TPU:513, one launch (start us, length us, event | category | flops | bytes accessed | tf_op | source)
XLA Modules:
  0.0 58.1 jit_solution(13813097922126324246)
XLA Ops:
  0.0 20.4 %collective-permute-start = (bf16[1,2,128]{2,1,0:T(2,128)(2,1)}, bf16[1,2,128]{2,1,0:T(2,128)(2,1)S(1)}, u32[]{:S(2)}, u32[]{:S(2)}) collective-permute-start(bf16[1,2,128]{2,1,0:T(2,128)(2,1)} %bitcast.21), channel_id=1, source_target_pairs={{0,1},{1,0},{2,3},{3,2},{4,5},{5,4},{6,7},{7,6},{8,9},{9,8},{10,11... | collective-permute-start | bytes 1544 | tf_op jit(solution)/shard_map/ppermute | solution.py:243
  20.4 0.0 collective-permute-start.1
  20.4 0.7 %pad_maximum_fusion.query_ref = bf16[1,2,192]{2,1,0:T(2,128)(2,1)S(1)} fusion(bf16[1,2,64]{2,1,0:T(2,128)(2,1)} %bitcast.20, bf16[1,2,128]{2,1,0:T(2,128)(2,1)} %bitcast.22), kind=kLoop, calls=%fused_computation | loop fusion | flops 1536 | bytes 1536 | tf_op jit(solution)/shard_map/concatenate | solution.py:266
  21.1 0.6 %collective-permute-done.1.far_rope_ref = bf16[1,2,64]{2,1,0:T(2,128)(2,1)S(1)} collective-permute-done((bf16[1,2,64]{2,1,0:T(2,128)(2,1)}, bf16[1,2,64]{2,1,0:T(2,128)(2,1)S(1)}, u32[]{:S(2)}, u32[]{:S(2)}) %collective-permute-start.1) | collective-permute-done | bytes 288 | tf_op jit(solution)/shard_map/ppermute | solution.py:243
  21.7 0.0 collective-permute-done.far_nope_ref
  21.7 0.0 copy-start
  21.7 0.0 copy-start.1
  21.7 0.0 copy-start.3
  21.7 0.0 copy-start.6
  21.7 0.0 copy-start.7
  21.7 0.0 copy-start.8
  21.8 16.1 %all_to_all.10 = bf16[64,4,128]{2,1,0:T(4,128)(2,1)S(1)} all-to-all(bf16[64,4,128]{2,1,0:T(4,128)(2,1)S(1)} %bitcast.16), channel_id=1, replica_groups=mesh['groups'=2,'chips'=64,'cores'=2] {'chips'}, dimensions={0} | all-to-all | bytes 131072 | tf_op jit(solution)/shard_map/all_to_all | solution.py:239
  37.9 0.0 copy-done
  37.9 0.0 copy-done.1
  37.9 0.0 copy-done.3
  37.9 0.0 copy-done.6
  37.9 0.0 copy-done.7
  37.9 0.0 copy-done.8
  38.0 0.0 copy-start.2
  38.0 0.0 copy-start.4
  38.0 0.0 copy-start.5
  38.0 1.6 %shard_map.111 = (f32[16,128]{1,0:T(8,128)S(1)}, f32[16,128]{1,0:T(8,128)S(1)}) custom-call(s32[1]{0:T(128)} %bitcast.idx_ref, s32[1,8]{1,0:T(1,128)S(1)} %bitcast.17, bf16[256,128]{1,0:T(8,128)(2,1)S(1)} %bitcast.13, bf16[2,16,128,512]{3,2,1,0:T(8,128)(2,1)S(1)} %copy-done, bf16[2,16,512,128]{3,2,1,0:T(8,128)(2,1)S(1)} %copy-done.1, ...), custom_call_target="tpu_custom_call" | custom-call | flops 16777216 | bytes 1048576 | tf_op jit(solution)/shard_map/pallas_call | solution.py:273
  39.6 1.5 %collective-permute-start.2 = (f32[16,128]{1,0:T(8,128)S(1)}, f32[16,128]{1,0:T(8,128)S(1)}, u32[]{:S(2)}, u32[]{:S(2)}) collective-permute-start(f32[16,128]{1,0:T(8,128)S(1)} %get-tuple-element.11), channel_id=1, source_target_pairs={{0,1},{1,0},{2,3},{3,2},{4,5},{5,4},{6,7},{7,6},{8,9},{9,8},{10,11... | collective-permute-start | bytes 24584 | tf_op jit(solution)/shard_map/ppermute | solution.py:243
  41.1 0.0 copy-done.2
  41.1 0.0 copy-done.4
  41.1 0.0 copy-done.5
  41.1 0.7 %shard_map.109 = (f32[8,128]{1,0:T(8,128)S(1)}, s32[16,128]{1,0:T(8,128)S(1)}) custom-call(s32[1]{0:T(128)} %bitcast.idx_ref, s32[1,8]{1,0:T(1,128)S(1)} %bitcast.18, bf16[1,2,192]{2,1,0:T(2,128)(2,1)S(1)} %pad_maximum_fusion.query_ref, bf16[2,16,128,512]{3,2,1,0:T(8,128)(2,1)S(1)} %copy-done, bf16[2,16,512,128]{3,2,1,0:T(8,128)(2,1)S(1)} %copy-done.1, ...), custom_call_target="tpu_custom_call" | custom-call | flops 16777216 | bytes 1048576 | tf_op jit(solution)/shard_map/pallas_call | solution.py:281
  41.8 0.1 collective-permute-done.2.far_ref
  41.9 15.5 %all_to_all.11 = f32[64,2,128]{2,1,0:T(2,128)S(1)} all-to-all(f32[64,2,128]{2,1,0:T(2,128)S(1)} %bitcast.15), channel_id=1, replica_groups=mesh['groups'=2,'chips'=64,'cores'=2] {'chips'}, dimensions={0} | all-to-all | bytes 131072 | tf_op jit(solution)/shard_map/all_to_all | solution.py:239
  57.5 0.6 %shard_map.113 = bf16[1,2,128]{2,1,0:T(2,128)(2,1)} custom-call(s32[16,128]{1,0:T(8,128)S(1)} %get-tuple-element.9.chips_ref, f32[128,128]{1,0:T(8,128)S(1)} %bitcast.14, f32[8,128]{1,0:T(8,128)S(1)} %get-tuple-element.12.aux_ref), custom_call_target="tpu_custom_call" | custom-call | flops 1048576 | bytes 1048576 | tf_op jit(solution)/shard_map/pallas_call | solution.py:293
  (2 shorter events, 0.1 us)
Async XLA Ops:
  0.0 21.7 %collective-permute-start = (bf16[1,2,128]{2,1,0:T(2,128)(2,1)}, bf16[1,2,128]{2,1,0:T(2,128)(2,1)S(1)}, u32[]{:S(2)}, u32[]{:S(2)}) collective-permute-start(bf16[1,2,128]{2,1,0:T(2,128)(2,1)} %bitcast.21), channel_id=1, source_target_pairs={{0,1},{1,0},{2,3},{3,2},{4,5},{5,4},{6,7},{7,6},{8,9},{9,8},{10,11... | collective-permute-start | bytes 1544 | tf_op jit(solution)/shard_map/ppermute | solution.py:243
  20.4 1.3 %collective-permute-start.1 = (bf16[1,2,64]{2,1,0:T(2,128)(2,1)}, bf16[1,2,64]{2,1,0:T(2,128)(2,1)S(1)}, u32[]{:S(2)}, u32[]{:S(2)}) collective-permute-start(bf16[1,2,64]{2,1,0:T(2,128)(2,1)} %bitcast.19), channel_id=1, source_target_pairs={{0,1},{1,0},{2,3},{3,2},{4,5},{5,4},{6,7},{7,6},{8,9},{9,8},{10,11... | collective-permute-start | bytes 776 | tf_op jit(solution)/shard_map/ppermute | solution.py:243
  21.7 16.2 %copy-start = (bf16[2,16,128,512]{3,2,1,0:T(8,128)(2,1)S(1)}, bf16[2,16,128,512]{3,2,1,0:T(8,128)(2,1)}, u32[]{:S(2)}) copy-start(bf16[2,16,128,512]{3,2,1,0:T(8,128)(2,1)} %w_uk_ref.3) | copy-start | bytes 12582916
  21.7 16.2 %copy-start.1 = (bf16[2,16,512,128]{3,2,1,0:T(8,128)(2,1)S(1)}, bf16[2,16,512,128]{3,2,1,0:T(8,128)(2,1)}, u32[]{:S(2)}) copy-start(bf16[2,16,512,128]{3,2,1,0:T(8,128)(2,1)} %w_uv_ref.3) | copy-start | bytes 12582916
  21.7 16.2 %copy-start.3 = (bf16[1,1,512,576]{2,3,1,0:T(8,128)(2,1)S(1)}, bf16[1,1,512,576]{2,3,1,0:T(8,128)(2,1)}, u32[]{:S(2)}) copy-start(bf16[1,1,512,576]{2,3,1,0:T(8,128)(2,1)} %param.16) | copy-start | bytes 1769476
  21.7 16.2 %copy-start.6 = (s32[8]{0:T(128)S(1)}, s32[8]{0:T(128)}, u32[]{:S(2)}) copy-start(s32[8]{0:T(128)} %param.21) | copy-start | bytes 100
  21.7 16.2 %copy-start.7 = (s32[1,128]{1,0:T(1,128)S(1)}, s32[1,128]{1,0:T(1,128)}, u32[]{:S(2)}) copy-start(s32[1,128]{1,0:T(1,128)} %map_ref.3) | copy-start | bytes 1540
  21.7 16.2 %copy-start.8 = (s32[1,1,512]{2,1,0:T(1,128)S(1)}, s32[1,1,512]{2,1,0:T(1,128)}, u32[]{:S(2)}) copy-start(s32[1,1,512]{2,1,0:T(1,128)} %slab_pos_ref.1) | copy-start | bytes 6148
  38.0 3.1 %copy-start.2 = (bf16[1,8,256,576]{2,3,1,0:T(8,128)(2,1)S(1)}, bf16[1,8,256,576]{2,3,1,0:T(8,128)(2,1)}, u32[]{:S(2)}) copy-start(bf16[1,8,256,576]{2,3,1,0:T(8,128)(2,1)} %param.19) | copy-start | bytes 7077892
  38.0 3.1 %copy-start.4 = (bf16[2,8,576]{2,1,0:T(8,128)(2,1)S(1)}, bf16[2,8,576]{2,1,0:T(8,128)(2,1)}, u32[]{:S(2)}) copy-start(bf16[2,8,576]{2,1,0:T(8,128)(2,1)} %newlat_ref.1) | copy-start | bytes 55300
  38.0 3.1 %copy-start.5 = (s32[1,8,256]{2,1,0:T(8,128)S(1)}, s32[1,8,256]{2,1,0:T(8,128)}, u32[]{:S(2)}) copy-start(s32[1,8,256]{2,1,0:T(8,128)} %deep_pos_ref.1) | copy-start | bytes 24580
  39.6 2.3 %collective-permute-start.2 = (f32[16,128]{1,0:T(8,128)S(1)}, f32[16,128]{1,0:T(8,128)S(1)}, u32[]{:S(2)}, u32[]{:S(2)}) collective-permute-start(f32[16,128]{1,0:T(8,128)S(1)} %get-tuple-element.11), channel_id=1, source_target_pairs={{0,1},{1,0},{2,3},{3,2},{4,5},{5,4},{6,7},{7,6},{8,9},{9,8},{10,11... | collective-permute-start | bytes 24584 | tf_op jit(solution)/shard_map/ppermute | solution.py:243

commit v7 on v6

--- a/solution.py
+++ b/solution.py
@@ -59,9 +59,20 @@
 
 
 def by_head(rows):
-    wide = jnp.concatenate([rows] * HEADS, axis=1)
+    wide = jnp.concatenate([rows] * rows.shape[0], axis=1)
     diagonal = iota(wide.shape, 1) // rows.shape[1] == iota(wide.shape, 0)
     return jnp.where(diagonal, wide, jnp.zeros_like(wide))
+
+
+def up_projected(out, w_uv_ref, parity):
+    half = HEADS // CORES
+    wide = jnp.concatenate([out] * half, axis=1)
+    row = iota(wide.shape, 0)
+    place = (iota(wide.shape, 1) // LATENT == row // CORES) & (row % CORES == parity)
+    heads = [w_uv_ref[0, k * CORES + parity] for k in range(half)]
+    return nn_dot(
+        jnp.where(place, wide, jnp.zeros_like(wide)), jnp.concatenate(heads, axis=0)
+    )
 
 
 def slab_request(map_ref, slot):
@@ -87,8 +98,9 @@
     map_ref,
     keep_ref,
     give_ref,
-    up_ref,
     level_ref,
+    rows_ref,
+    all_level_ref,
 ):
     holder = idx_ref[0]
     core = holder % CORES
@@ -115,12 +127,14 @@
     out = nt_dot(weight, latent) / safe
     level = jnp.where(total > 0.0, top + jnp.log(safe), neg_fill)
 
-    up_ref[...] = nn_dot(by_head(out.astype(bf16)), w_uv_ref[0].reshape(-1, LANES))
-    level_ref[...] = jnp.broadcast_to(level, level_ref.shape)
+    out = out.astype(bf16)
+    keep_ref[...] = out
+    rows_ref[...] = up_projected(out, w_uv_ref, 1 - core)
+    all_level_ref[...] = jnp.broadcast_to(level, all_level_ref.shape)
     half = HEADS // CORES
-    for ref, first in ((keep_ref, core), (give_ref, 1 - core)):
-        ref[:half] = up_ref[pl.ds(first, half, stride=CORES), :]
-        ref[half:] = level_ref[pl.ds(first, half, stride=CORES), :]
+    give_ref[:half] = rows_ref[pl.ds(1 - core, half, stride=CORES), :]
+    give_ref[half:] = all_level_ref[pl.ds(1 - core, half, stride=CORES), :]
+    level_ref[...] = all_level_ref[pl.ds(core, half, stride=CORES), :]
 
 
 def own_kernel(
@@ -133,8 +147,11 @@
     map_ref,
     deep_ref,
     deep_pos_ref,
+    keep_ref,
     aux_ref,
     chips_ref,
+    up_ref,
+    rows_ref,
 ):
     holder = idx_ref[0]
     own_req = holder // HEADS
@@ -175,16 +192,20 @@
         req = slab_request(map_ref, slot).astype(f32)
         aux_ref[row : row + 1, :] = jnp.broadcast_to(req, (1, LANES))
 
+    core = holder % CORES
+    rows_ref[...] = up_projected(keep_ref[...], w_uv_ref, core)
+    up_ref[...] = rows_ref[pl.ds(core, HEADS // CORES, stride=CORES), :]
+
     shape = chips_ref.shape
     place = iota(shape, 1) == own_req * SLABS_REQ + iota(shape, 0)
     slots = jnp.sum(jnp.where(place, map_ref[...], 0), axis=1, keepdims=True)
     chips_ref[...] = jnp.broadcast_to(slots // CORES, shape)
 
 
-def merge_kernel(keep_ref, far_ref, aux_ref, send_ref):
+def merge_kernel(near_ref, near_level_ref, far_ref, aux_ref, send_ref):
     near_req, far_req = aux_ref[3:4, :], aux_ref[4:5, :]
-    half = keep_ref.shape[0] // 2
-    near, near_level = keep_ref[:half], keep_ref[half:]
+    half = near_ref.shape[0]
+    near, near_level = near_ref[...], near_level_ref[...]
     far, far_level = far_ref[:half], far_ref[half:]
     top = jnp.maximum(near_level, far_level)
     near_factor, far_factor = jnp.exp(near_level - top), jnp.exp(far_level - top)
@@ -268,26 +289,35 @@
         prep_kernel, shape((chips * CORES * 2, LANES), bf16), [SMEM] + [VMEM] * 3, 1 << 33
     )(holder, query, far_nope, far_rope)
     queries = exchanged(queries, CORES * 2)
-    block = shape((HEADS // CORES * MSG, LANES), f32)
+    half = HEADS // CORES
     lengths = lengths.reshape(1, -1)
-    keep, give = call(
+    keep, give, level = call(
         attend_kernel,
-        (block, block),
+        (
+            shape((HEADS, LATENT), bf16),
+            shape((half * MSG, LANES), f32),
+            shape((half, LANES), f32),
+        ),
         [SMEM] + [VMEM] * 7,
         1 << 24,
         [pltpu.VMEM((HEADS, LANES), f32)] * 2,
     )(holder, lengths, queries, w_uk, w_uv, shallow_cache, slot_positions, slab_map)
     far = swapped(give)
-    aux, slab_chips = call(
+    aux, slab_chips, near = call(
         own_kernel,
-        (shape((8, LANES), f32), shape((SLABS_REQ, LANES), jnp.int32)),
-        [SMEM] + [VMEM] * 8,
+        (
+            shape((8, LANES), f32),
+            shape((SLABS_REQ, LANES), jnp.int32),
+            shape((half, LANES), f32),
+        ),
+        [SMEM] + [VMEM] * 9,
         1 << 24,
+        [pltpu.VMEM((HEADS, LANES), f32)],
     )(
-        holder, lengths, query, w_uk, w_uv, new_latent, slab_map, deep_cache, deep_positions
-    )
-    partials = call(merge_kernel, shape((chips * MSG, LANES), f32), [VMEM] * 3, 1 << 20)(
-        keep, far, aux
+        holder, lengths, query, w_uk, w_uv, new_latent, slab_map, deep_cache, deep_positions, keep
+    )
+    partials = call(merge_kernel, shape((chips * MSG, LANES), f32), [VMEM] * 4, 1 << 20)(
+        near, level, far, aux
     )
     partials = exchanged(partials, MSG)
     rows = call(combine_kernel, shape(q_nope.shape, bf16), [VMEM] * 3, 1 << 20)(

time: 58.2 us -> 58.2 us (level)
  transfers between devices with their start and end apart: 3 -> 3, of which waited for: 2 -> 1; matrix products, arithmetic and copies ran while one was open for 1% -> 1% of each run, Pallas kernels for 1% -> 1%
where the time goes in v7:
time: 58.2 us; the launch traced here: 58 us
  blocking collectives  31.6 us (54%)
  starting transfers between devices  21.9 us (38%)
  Pallas kernels  3 us (5%)
  other arithmetic  0.68 us (1%)
  waiting for transfers between devices  0.62 us (1%)
    all_to_all x2, blocking collectives, exchanged(): return lax.all_to_all(tiles, 'chips', 0, 0, tiled=True).reshape(rows.shape)  31.6 us
    ppermute x3, starting transfers between devices, swapped(): lax.ppermute(x, 'cores', [(k, (k + 1) % CORES) for k in range(CORES)])  21.9 us
    pallas_call x1, Pallas kernels, shards(): call(attend_kernel, (shape((HEADS, LATENT), bf16), shape((half * MSG, LAN...  1.47 us
  transfers between devices with their start and end apart: 3, of which 1 were waited for; matrix products, arithmetic and copies ran while one was open for 1% of the time, Pallas kernels for 1%

profile of v7, /device:TPU:513, one launch (start us, length us, event | category | flops | bytes accessed | tf_op | source)
XLA Modules:
  0.0 58.0 jit_solution(7880627259981767661)
XLA Ops:
  0.0 20.4 %collective-permute-start = (bf16[1,2,128]{2,1,0:T(2,128)(2,1)}, bf16[1,2,128]{2,1,0:T(2,128)(2,1)S(1)}, u32[]{:S(2)}, u32[]{:S(2)}) collective-permute-start(bf16[1,2,128]{2,1,0:T(2,128)(2,1)} %bitcast.21), channel_id=1, source_target_pairs={{0,1},{1,0},{2,3},{3,2},{4,5},{5,4},{6,7},{7,6},{8,9},{9,8},{10,11... | collective-permute-start | bytes 1544 | tf_op jit(solution)/shard_map/ppermute | solution.py:264
  20.4 0.0 collective-permute-start.1
  20.4 0.7 %pad_maximum_fusion.query_ref = bf16[1,2,192]{2,1,0:T(2,128)(2,1)S(1)} fusion(bf16[1,2,64]{2,1,0:T(2,128)(2,1)} %bitcast.20, bf16[1,2,128]{2,1,0:T(2,128)(2,1)} %bitcast.22), kind=kLoop, calls=%fused_computation | loop fusion | flops 1536 | bytes 1536 | tf_op jit(solution)/shard_map/concatenate | solution.py:287
  21.1 0.6 %collective-permute-done.1.far_rope_ref = bf16[1,2,64]{2,1,0:T(2,128)(2,1)S(1)} collective-permute-done((bf16[1,2,64]{2,1,0:T(2,128)(2,1)}, bf16[1,2,64]{2,1,0:T(2,128)(2,1)S(1)}, u32[]{:S(2)}, u32[]{:S(2)}) %collective-permute-start.1) | collective-permute-done | bytes 288 | tf_op jit(solution)/shard_map/ppermute | solution.py:264
  21.7 0.0 collective-permute-done.far_nope_ref
  21.7 0.0 copy-start
  21.7 0.0 copy-start.1
  21.7 0.0 copy-start.3
  21.7 0.0 copy-start.6
  21.7 0.0 copy-start.7
  21.7 0.0 copy-start.8
  21.8 16.1 %all_to_all.10 = bf16[64,4,128]{2,1,0:T(4,128)(2,1)S(1)} all-to-all(bf16[64,4,128]{2,1,0:T(4,128)(2,1)S(1)} %bitcast.16), channel_id=1, replica_groups=mesh['groups'=2,'chips'=64,'cores'=2] {'chips'}, dimensions={0} | all-to-all | bytes 131072 | tf_op jit(solution)/shard_map/all_to_all | solution.py:260
  37.9 0.0 copy-done
  37.9 0.0 copy-done.1
  37.9 0.0 copy-done.3
  37.9 0.0 copy-done.6
  37.9 0.0 copy-done.7
  37.9 0.0 copy-done.8
  38.0 0.0 copy-start.2
  38.0 0.0 copy-start.4
  38.0 0.0 copy-start.5
  38.0 1.5 %shard_map.110 = (bf16[16,512]{1,0:T(8,128)(2,1)S(1)}, f32[16,128]{1,0:T(8,128)S(1)}, f32[8,128]{1,0:T(8,128)S(1)}) custom-call(s32[1]{0:T(128)} %bitcast.idx_ref, s32[1,8]{1,0:T(1,128)S(1)} %bitcast.17, bf16[256,128]{1,0:T(8,128)(2,1)S(1)} %bitcast.13, bf16[2,16,128,512]{3,2,1,0:T(8,128)(2,1)S(1)} %copy-done, bf16[2,16,512,128]{3,2,1,0:T(8,128)(2,1)S(1)} %copy-done.1, ...), custom_call_target="tpu_custom_call" | custom-call | flops 16777216 | bytes 1048576 | tf_op jit(solution)/shard_map/pallas_call | solution.py:294
  39.5 1.5 %collective-permute-start.2 = (f32[16,128]{1,0:T(8,128)S(1)}, f32[16,128]{1,0:T(8,128)S(1)}, u32[]{:S(2)}, u32[]{:S(2)}) collective-permute-start(f32[16,128]{1,0:T(8,128)S(1)} %get-tuple-element.15), channel_id=1, source_target_pairs={{0,1},{1,0},{2,3},{3,2},{4,5},{5,4},{6,7},{7,6},{8,9},{9,8},{10,11... | collective-permute-start | bytes 24584 | tf_op jit(solution)/shard_map/ppermute | solution.py:264
  41.0 0.0 copy-done.2
  41.0 0.0 copy-done.4
  41.0 0.0 copy-done.5
  41.0 0.9 %shard_map.111 = (f32[8,128]{1,0:T(8,128)S(1)}, s32[16,128]{1,0:T(8,128)S(1)}, f32[8,128]{1,0:T(8,128)S(1)}) custom-call(s32[1]{0:T(128)} %bitcast.idx_ref, s32[1,8]{1,0:T(1,128)S(1)} %bitcast.18, bf16[1,2,192]{2,1,0:T(2,128)(2,1)S(1)} %pad_maximum_fusion.query_ref, bf16[2,16,128,512]{3,2,1,0:T(8,128)(2,1)S(1)} %copy-done, ...), custom_call_target="tpu_custom_call" | custom-call | flops 16777216 | bytes 1048576 | tf_op jit(solution)/shard_map/pallas_call | solution.py:306
  41.8 0.0 collective-permute-done.2.far_ref
  41.9 15.5 %all_to_all.11 = f32[64,2,128]{2,1,0:T(2,128)S(1)} all-to-all(f32[64,2,128]{2,1,0:T(2,128)S(1)} %bitcast.15), channel_id=1, replica_groups=mesh['groups'=2,'chips'=64,'cores'=2] {'chips'}, dimensions={0} | all-to-all | bytes 131072 | tf_op jit(solution)/shard_map/all_to_all | solution.py:260
  57.4 0.6 %shard_map.113 = bf16[1,2,128]{2,1,0:T(2,128)(2,1)} custom-call(s32[16,128]{1,0:T(8,128)S(1)} %get-tuple-element.12.chips_ref, f32[128,128]{1,0:T(8,128)S(1)} %bitcast.14, f32[8,128]{1,0:T(8,128)S(1)} %get-tuple-element.16.aux_ref), custom_call_target="tpu_custom_call" | custom-call | flops 1048576 | bytes 1048576 | tf_op jit(solution)/shard_map/pallas_call | solution.py:323
  (2 shorter events, 0.1 us)
Async XLA Ops:
  0.0 21.7 %collective-permute-start = (bf16[1,2,128]{2,1,0:T(2,128)(2,1)}, bf16[1,2,128]{2,1,0:T(2,128)(2,1)S(1)}, u32[]{:S(2)}, u32[]{:S(2)}) collective-permute-start(bf16[1,2,128]{2,1,0:T(2,128)(2,1)} %bitcast.21), channel_id=1, source_target_pairs={{0,1},{1,0},{2,3},{3,2},{4,5},{5,4},{6,7},{7,6},{8,9},{9,8},{10,11... | collective-permute-start | bytes 1544 | tf_op jit(solution)/shard_map/ppermute | solution.py:264
  20.4 1.3 %collective-permute-start.1 = (bf16[1,2,64]{2,1,0:T(2,128)(2,1)}, bf16[1,2,64]{2,1,0:T(2,128)(2,1)S(1)}, u32[]{:S(2)}, u32[]{:S(2)}) collective-permute-start(bf16[1,2,64]{2,1,0:T(2,128)(2,1)} %bitcast.19), channel_id=1, source_target_pairs={{0,1},{1,0},{2,3},{3,2},{4,5},{5,4},{6,7},{7,6},{8,9},{9,8},{10,11... | collective-permute-start | bytes 776 | tf_op jit(solution)/shard_map/ppermute | solution.py:264
  21.7 16.2 %copy-start = (bf16[2,16,128,512]{3,2,1,0:T(8,128)(2,1)S(1)}, bf16[2,16,128,512]{3,2,1,0:T(8,128)(2,1)}, u32[]{:S(2)}) copy-start(bf16[2,16,128,512]{3,2,1,0:T(8,128)(2,1)} %w_uk_ref.3) | copy-start | bytes 12582916
  21.7 16.2 %copy-start.1 = (bf16[2,16,512,128]{3,2,1,0:T(8,128)(2,1)S(1)}, bf16[2,16,512,128]{3,2,1,0:T(8,128)(2,1)}, u32[]{:S(2)}) copy-start(bf16[2,16,512,128]{3,2,1,0:T(8,128)(2,1)} %w_uv_ref.3) | copy-start | bytes 12582916
  21.7 16.2 %copy-start.3 = (bf16[1,1,512,576]{2,3,1,0:T(8,128)(2,1)S(1)}, bf16[1,1,512,576]{2,3,1,0:T(8,128)(2,1)}, u32[]{:S(2)}) copy-start(bf16[1,1,512,576]{2,3,1,0:T(8,128)(2,1)} %param.16) | copy-start | bytes 1769476
  21.7 16.2 %copy-start.6 = (s32[8]{0:T(128)S(1)}, s32[8]{0:T(128)}, u32[]{:S(2)}) copy-start(s32[8]{0:T(128)} %param.21) | copy-start | bytes 100
  21.7 16.2 %copy-start.7 = (s32[1,128]{1,0:T(1,128)S(1)}, s32[1,128]{1,0:T(1,128)}, u32[]{:S(2)}) copy-start(s32[1,128]{1,0:T(1,128)} %map_ref.3) | copy-start | bytes 1540
  21.7 16.2 %copy-start.8 = (s32[1,1,512]{2,1,0:T(1,128)S(1)}, s32[1,1,512]{2,1,0:T(1,128)}, u32[]{:S(2)}) copy-start(s32[1,1,512]{2,1,0:T(1,128)} %slab_pos_ref.1) | copy-start | bytes 6148
  38.0 3.0 %copy-start.2 = (bf16[1,8,256,576]{2,3,1,0:T(8,128)(2,1)S(1)}, bf16[1,8,256,576]{2,3,1,0:T(8,128)(2,1)}, u32[]{:S(2)}) copy-start(bf16[1,8,256,576]{2,3,1,0:T(8,128)(2,1)} %param.19) | copy-start | bytes 7077892
  38.0 3.0 %copy-start.4 = (bf16[2,8,576]{2,1,0:T(8,128)(2,1)S(1)}, bf16[2,8,576]{2,1,0:T(8,128)(2,1)}, u32[]{:S(2)}) copy-start(bf16[2,8,576]{2,1,0:T(8,128)(2,1)} %newlat_ref.1) | copy-start | bytes 55300
  38.0 3.0 %copy-start.5 = (s32[1,8,256]{2,1,0:T(8,128)S(1)}, s32[1,8,256]{2,1,0:T(8,128)}, u32[]{:S(2)}) copy-start(s32[1,8,256]{2,1,0:T(8,128)} %deep_pos_ref.1) | copy-start | bytes 24580
  39.5 2.4 %collective-permute-start.2 = (f32[16,128]{1,0:T(8,128)S(1)}, f32[16,128]{1,0:T(8,128)S(1)}, u32[]{:S(2)}, u32[]{:S(2)}) collective-permute-start(f32[16,128]{1,0:T(8,128)S(1)} %get-tuple-element.15), channel_id=1, source_target_pairs={{0,1},{1,0},{2,3},{3,2},{4,5},{5,4},{6,7},{7,6},{8,9},{9,8},{10,11... | collective-permute-start | bytes 24584 | tf_op jit(solution)/shard_map/ppermute | solution.py:264

commit v8 on v7

--- a/solution.py
+++ b/solution.py
@@ -120,8 +120,9 @@
     rotary = slab_ref[0, 0, LATENT:]
     score = (nn_dot(q_lat, latent) + nn_dot(q_rope, rotary)) * score_scale
     live = slab_pos_ref[0] < length_of(lengths_ref, req_v)
-    top = jnp.max(jnp.where(live, score, neg_fill), axis=1, keepdims=True)
-    weight = jnp.where(live, jnp.exp(jnp.where(live, score - top, 0.0)), 0.0).astype(bf16)
+    score = jnp.where(live, score, neg_fill)
+    top = jnp.max(score, axis=1, keepdims=True)
+    weight = jnp.where(live, jnp.exp(score - top), 0.0).astype(bf16)
     total = jnp.sum(weight.astype(f32), axis=1, keepdims=True)
     safe = jnp.where(total > 0.0, total, 1.0)
     out = nt_dot(weight, latent) / safe
@@ -172,8 +173,9 @@
     rotary = deep_ref[0, own_req, LATENT:]
     score = (nn_dot(own_lat, latent) + nn_dot(rope[1:], rotary)) * score_scale
     live = deep_pos_ref[0, pl.ds(own_req, 1), :] < length_of(lengths_ref, own_req)
-    block_max = jnp.max(jnp.where(live, score, neg_fill), axis=1, keepdims=True)
-    weight = jnp.where(live, jnp.exp(jnp.where(live, score - block_max, 0.0)), 0.0).astype(bf16)
+    score = jnp.where(live, score, neg_fill)
+    block_max = jnp.max(score, axis=1, keepdims=True)
+    weight = jnp.where(live, jnp.exp(score - block_max), 0.0).astype(bf16)
     block_sum = jnp.sum(weight.astype(f32), axis=1, keepdims=True)
     block_out = nt_dot(weight, latent)
     newlat = picked_row(newlat_ref[1], own_req)

time: 58.2 us -> 58.2 us (level)
  no operation moved by 1% of the time
where the time goes in v8:
time: 58.2 us; the launch traced here: 58 us
  blocking collectives  31.6 us (54%)
  starting transfers between devices  21.9 us (38%)
  Pallas kernels  3 us (5%)
  other arithmetic  0.68 us (1%)
  waiting for transfers between devices  0.62 us (1%)
    all_to_all x2, blocking collectives, exchanged(): return lax.all_to_all(tiles, 'chips', 0, 0, tiled=True).reshape(rows.shape)  31.6 us
    ppermute x3, starting transfers between devices, swapped(): lax.ppermute(x, 'cores', [(k, (k + 1) % CORES) for k in range(CORES)])  21.9 us
    pallas_call x1, Pallas kernels, shards(): call(attend_kernel, (shape((HEADS, LATENT), bf16), shape((half * MSG, LAN...  1.47 us
  transfers between devices with their start and end apart: 3, of which 1 were waited for; matrix products, arithmetic and copies ran while one was open for 1% of the time, Pallas kernels for 1%

profile of v8, /device:TPU:513, one launch (start us, length us, event | category | flops | bytes accessed | tf_op | source)
XLA Modules:
  0.0 58.0 jit_solution(13124285663109686764)
XLA Ops:
  0.0 20.4 %collective-permute-start = (bf16[1,2,128]{2,1,0:T(2,128)(2,1)}, bf16[1,2,128]{2,1,0:T(2,128)(2,1)S(1)}, u32[]{:S(2)}, u32[]{:S(2)}) collective-permute-start(bf16[1,2,128]{2,1,0:T(2,128)(2,1)} %bitcast.21), channel_id=1, source_target_pairs={{0,1},{1,0},{2,3},{3,2},{4,5},{5,4},{6,7},{7,6},{8,9},{9,8},{10,11... | collective-permute-start | bytes 1544 | tf_op jit(solution)/shard_map/ppermute | solution.py:266
  20.4 0.0 collective-permute-start.1
  20.4 0.7 %pad_maximum_fusion.query_ref = bf16[1,2,192]{2,1,0:T(2,128)(2,1)S(1)} fusion(bf16[1,2,64]{2,1,0:T(2,128)(2,1)} %bitcast.20, bf16[1,2,128]{2,1,0:T(2,128)(2,1)} %bitcast.22), kind=kLoop, calls=%fused_computation | loop fusion | flops 1536 | bytes 1536 | tf_op jit(solution)/shard_map/concatenate | solution.py:289
  21.1 0.6 %collective-permute-done.1.far_rope_ref = bf16[1,2,64]{2,1,0:T(2,128)(2,1)S(1)} collective-permute-done((bf16[1,2,64]{2,1,0:T(2,128)(2,1)}, bf16[1,2,64]{2,1,0:T(2,128)(2,1)S(1)}, u32[]{:S(2)}, u32[]{:S(2)}) %collective-permute-start.1) | collective-permute-done | bytes 288 | tf_op jit(solution)/shard_map/ppermute | solution.py:266
  21.7 0.0 collective-permute-done.far_nope_ref
  21.7 0.0 copy-start
  21.7 0.0 copy-start.1
  21.7 0.0 copy-start.3
  21.7 0.0 copy-start.6
  21.7 0.0 copy-start.7
  21.7 0.0 copy-start.8
  21.8 16.1 %all_to_all.10 = bf16[64,4,128]{2,1,0:T(4,128)(2,1)S(1)} all-to-all(bf16[64,4,128]{2,1,0:T(4,128)(2,1)S(1)} %bitcast.16), channel_id=1, replica_groups=mesh['groups'=2,'chips'=64,'cores'=2] {'chips'}, dimensions={0} | all-to-all | bytes 131072 | tf_op jit(solution)/shard_map/all_to_all | solution.py:262
  37.9 0.0 copy-done
  37.9 0.0 copy-done.1
  37.9 0.0 copy-done.3
  37.9 0.0 copy-done.6
  37.9 0.0 copy-done.7
  37.9 0.0 copy-done.8
  38.0 0.0 copy-start.2
  38.0 0.0 copy-start.4
  38.0 0.0 copy-start.5
  38.0 1.5 %shard_map.110 = (bf16[16,512]{1,0:T(8,128)(2,1)S(1)}, f32[16,128]{1,0:T(8,128)S(1)}, f32[8,128]{1,0:T(8,128)S(1)}) custom-call(s32[1]{0:T(128)} %bitcast.idx_ref, s32[1,8]{1,0:T(1,128)S(1)} %bitcast.17, bf16[256,128]{1,0:T(8,128)(2,1)S(1)} %bitcast.13, bf16[2,16,128,512]{3,2,1,0:T(8,128)(2,1)S(1)} %copy-done, bf16[2,16,512,128]{3,2,1,0:T(8,128)(2,1)S(1)} %copy-done.1, ...), custom_call_target="tpu_custom_call" | custom-call | flops 16777216 | bytes 1048576 | tf_op jit(solution)/shard_map/pallas_call | solution.py:296
  39.5 1.5 %collective-permute-start.2 = (f32[16,128]{1,0:T(8,128)S(1)}, f32[16,128]{1,0:T(8,128)S(1)}, u32[]{:S(2)}, u32[]{:S(2)}) collective-permute-start(f32[16,128]{1,0:T(8,128)S(1)} %get-tuple-element.15), channel_id=1, source_target_pairs={{0,1},{1,0},{2,3},{3,2},{4,5},{5,4},{6,7},{7,6},{8,9},{9,8},{10,11... | collective-permute-start | bytes 24584 | tf_op jit(solution)/shard_map/ppermute | solution.py:266
  41.0 0.0 copy-done.2
  41.0 0.0 copy-done.4
  41.0 0.0 copy-done.5
  41.0 0.9 %shard_map.111 = (f32[8,128]{1,0:T(8,128)S(1)}, s32[16,128]{1,0:T(8,128)S(1)}, f32[8,128]{1,0:T(8,128)S(1)}) custom-call(s32[1]{0:T(128)} %bitcast.idx_ref, s32[1,8]{1,0:T(1,128)S(1)} %bitcast.18, bf16[1,2,192]{2,1,0:T(2,128)(2,1)S(1)} %pad_maximum_fusion.query_ref, bf16[2,16,128,512]{3,2,1,0:T(8,128)(2,1)S(1)} %copy-done, ...), custom_call_target="tpu_custom_call" | custom-call | flops 16777216 | bytes 1048576 | tf_op jit(solution)/shard_map/pallas_call | solution.py:308
  41.8 0.0 collective-permute-done.2.far_ref
  41.9 15.5 %all_to_all.11 = f32[64,2,128]{2,1,0:T(2,128)S(1)} all-to-all(f32[64,2,128]{2,1,0:T(2,128)S(1)} %bitcast.15), channel_id=1, replica_groups=mesh['groups'=2,'chips'=64,'cores'=2] {'chips'}, dimensions={0} | all-to-all | bytes 131072 | tf_op jit(solution)/shard_map/all_to_all | solution.py:262
  57.4 0.6 %shard_map.113 = bf16[1,2,128]{2,1,0:T(2,128)(2,1)} custom-call(s32[16,128]{1,0:T(8,128)S(1)} %get-tuple-element.12.chips_ref, f32[128,128]{1,0:T(8,128)S(1)} %bitcast.14, f32[8,128]{1,0:T(8,128)S(1)} %get-tuple-element.16.aux_ref), custom_call_target="tpu_custom_call" | custom-call | flops 1048576 | bytes 1048576 | tf_op jit(solution)/shard_map/pallas_call | solution.py:325
  (2 shorter events, 0.1 us)
Async XLA Ops:
  0.0 21.7 %collective-permute-start = (bf16[1,2,128]{2,1,0:T(2,128)(2,1)}, bf16[1,2,128]{2,1,0:T(2,128)(2,1)S(1)}, u32[]{:S(2)}, u32[]{:S(2)}) collective-permute-start(bf16[1,2,128]{2,1,0:T(2,128)(2,1)} %bitcast.21), channel_id=1, source_target_pairs={{0,1},{1,0},{2,3},{3,2},{4,5},{5,4},{6,7},{7,6},{8,9},{9,8},{10,11... | collective-permute-start | bytes 1544 | tf_op jit(solution)/shard_map/ppermute | solution.py:266
  20.4 1.3 %collective-permute-start.1 = (bf16[1,2,64]{2,1,0:T(2,128)(2,1)}, bf16[1,2,64]{2,1,0:T(2,128)(2,1)S(1)}, u32[]{:S(2)}, u32[]{:S(2)}) collective-permute-start(bf16[1,2,64]{2,1,0:T(2,128)(2,1)} %bitcast.19), channel_id=1, source_target_pairs={{0,1},{1,0},{2,3},{3,2},{4,5},{5,4},{6,7},{7,6},{8,9},{9,8},{10,11... | collective-permute-start | bytes 776 | tf_op jit(solution)/shard_map/ppermute | solution.py:266
  21.7 16.2 %copy-start = (bf16[2,16,128,512]{3,2,1,0:T(8,128)(2,1)S(1)}, bf16[2,16,128,512]{3,2,1,0:T(8,128)(2,1)}, u32[]{:S(2)}) copy-start(bf16[2,16,128,512]{3,2,1,0:T(8,128)(2,1)} %w_uk_ref.3) | copy-start | bytes 12582916
  21.7 16.2 %copy-start.1 = (bf16[2,16,512,128]{3,2,1,0:T(8,128)(2,1)S(1)}, bf16[2,16,512,128]{3,2,1,0:T(8,128)(2,1)}, u32[]{:S(2)}) copy-start(bf16[2,16,512,128]{3,2,1,0:T(8,128)(2,1)} %w_uv_ref.3) | copy-start | bytes 12582916
  21.7 16.2 %copy-start.3 = (bf16[1,1,512,576]{2,3,1,0:T(8,128)(2,1)S(1)}, bf16[1,1,512,576]{2,3,1,0:T(8,128)(2,1)}, u32[]{:S(2)}) copy-start(bf16[1,1,512,576]{2,3,1,0:T(8,128)(2,1)} %param.16) | copy-start | bytes 1769476
  21.7 16.2 %copy-start.6 = (s32[8]{0:T(128)S(1)}, s32[8]{0:T(128)}, u32[]{:S(2)}) copy-start(s32[8]{0:T(128)} %param.21) | copy-start | bytes 100
  21.7 16.2 %copy-start.7 = (s32[1,128]{1,0:T(1,128)S(1)}, s32[1,128]{1,0:T(1,128)}, u32[]{:S(2)}) copy-start(s32[1,128]{1,0:T(1,128)} %map_ref.3) | copy-start | bytes 1540
  21.7 16.2 %copy-start.8 = (s32[1,1,512]{2,1,0:T(1,128)S(1)}, s32[1,1,512]{2,1,0:T(1,128)}, u32[]{:S(2)}) copy-start(s32[1,1,512]{2,1,0:T(1,128)} %slab_pos_ref.1) | copy-start | bytes 6148
  38.0 3.0 %copy-start.2 = (bf16[1,8,256,576]{2,3,1,0:T(8,128)(2,1)S(1)}, bf16[1,8,256,576]{2,3,1,0:T(8,128)(2,1)}, u32[]{:S(2)}) copy-start(bf16[1,8,256,576]{2,3,1,0:T(8,128)(2,1)} %param.19) | copy-start | bytes 7077892
  38.0 3.0 %copy-start.4 = (bf16[2,8,576]{2,1,0:T(8,128)(2,1)S(1)}, bf16[2,8,576]{2,1,0:T(8,128)(2,1)}, u32[]{:S(2)}) copy-start(bf16[2,8,576]{2,1,0:T(8,128)(2,1)} %newlat_ref.1) | copy-start | bytes 55300
  38.0 3.0 %copy-start.5 = (s32[1,8,256]{2,1,0:T(8,128)S(1)}, s32[1,8,256]{2,1,0:T(8,128)}, u32[]{:S(2)}) copy-start(s32[1,8,256]{2,1,0:T(8,128)} %deep_pos_ref.1) | copy-start | bytes 24580
  39.5 2.4 %collective-permute-start.2 = (f32[16,128]{1,0:T(8,128)S(1)}, f32[16,128]{1,0:T(8,128)S(1)}, u32[]{:S(2)}, u32[]{:S(2)}) collective-permute-start(f32[16,128]{1,0:T(8,128)S(1)} %get-tuple-element.15), channel_id=1, source_target_pairs={{0,1},{1,0},{2,3},{3,2},{4,5},{5,4},{6,7},{7,6},{8,9},{9,8},{10,11... | collective-permute-start | bytes 24584 | tf_op jit(solution)/shard_map/ppermute | solution.py:266
